TPU v7x, 32 devices: a whole 2x2x4 slice. The times are simulated.
32 devices in a mesh: gx: 4 (over y, x), gy: 4 (over z), gz: 2 (over core).
Axes of the slice: x: 2, y: 2, z: 4, core: 2. Of those that a mesh axis runs over, the one named last changes fastest.
Arguments:
- density: float32 [32, 256, 256], P('gx', 'gy', 'gz'), may hold values from 0.2 to 6, as said below
- momentum: float32 [3, 32, 256, 256], P(None, 'gx', 'gy', 'gz'), may hold values from -6 to 6
- energy: float32 [32, 256, 256], P('gx', 'gy', 'gz'), may hold values from 0.2 to 6, as said below
- displacement: int32 [3, 32, 256, 256], P(None, 'gx', 'gy', 'gz'), may hold values from -255 to 255
- flags: int32 [6], replicated, may hold values from 0 to 1
Outputs:
- new_density: float32 [32, 256, 256], P('gx', 'gy', 'gz')
- new_momentum: float32 [3, 32, 256, 256], P(None, 'gx', 'gy', 'gz')
- new_energy: float32 [32, 256, 256], P('gx', 'gy', 'gz')
- totals: float32 [2], replicated
Inputs may be any that keep to these rules, and one draw needn't show every extreme that they name: density is positive. energy is positive.
All inputs are finite; a program needn't handle non-finite values.
Results may differ from a plain program's by a relative error of at most 0.0003.
Values sent between devices are 32-bit elements; how exact they have to be, the bound alone decides.
A program may use at most 64 MiB of HBM per device.

v0:
```python
import jax
import jax.numpy as jnp
from jax import lax
from jax.sharding import PartitionSpec as P


def from_behind(value, axis, steps):
    count = lax.axis_size(axis)
    leading, last = (max(0, -steps), min(count, count - steps))
    return lax.ppermute(value, axis, [(source, source + steps) for source in range(leading, last)])


def padded_2(block, sides, width):
    for axis, dim in sides:
        count = lax.axis_size(axis)
        forward = [(i, i + 1) for i in range(count - 1)]
        backward = [(target, source) for source, target in forward]
        low = lax.ppermute(
            lax.slice_in_dim(block, block.shape[dim] - width, None, axis=dim), axis, forward
        )
        high = lax.ppermute(lax.slice_in_dim(block, 0, width, axis=dim), axis, backward)
        block = jnp.concatenate([low, block, high], axis=dim)
    return block


def minmod(left_diff, right_diff):
    return (
        0.5
        * (jnp.sign(left_diff) + jnp.sign(right_diff))
        * jnp.minimum(jnp.abs(left_diff), jnp.abs(right_diff))
    )


def flux_change(padded, face_rows, along):
    total_len = padded.shape[along]
    upper_cells = lax.slice_in_dim(padded, 2, total_len, axis=along)
    middle = lax.slice_in_dim(padded, 1, total_len - 1, axis=along)
    lower_cells = lax.slice_in_dim(padded, 0, total_len - 2, axis=along)
    slopes = minmod(upper_cells - middle, middle - lower_cells)
    k = total_len - 2
    low_val = lax.slice_in_dim(middle, 0, k - 1, axis=along)
    high_val = lax.slice_in_dim(middle, 1, k, axis=along)
    low_slope = lax.slice_in_dim(slopes, 0, k - 1, axis=along)
    high_slope = lax.slice_in_dim(slopes, 1, k, axis=along)
    fluxes = face_rows * jnp.where(
        face_rows > 0,
        low_val + 0.5 * (1.0 - face_rows) * low_slope,
        high_val - 0.5 * (1.0 + face_rows) * high_slope,
    )
    m = k - 1
    return lax.slice_in_dim(fluxes, 0, m - 1, axis=along) - lax.slice_in_dim(
        fluxes, 1, m, axis=along
    )


def fix_ghosts(padded, along, position, count_on):
    total_len = padded.shape[along]
    first_cell = lax.slice_in_dim(padded, 2, 3, axis=along)
    last_cell = lax.slice_in_dim(padded, total_len - 3, total_len - 2, axis=along)
    low_ghosts = jnp.where(
        position == 0,
        jnp.concatenate([first_cell, first_cell], along),
        lax.slice_in_dim(padded, 0, 2, axis=along),
    )
    high_ghosts = jnp.where(
        position == count_on - 1,
        jnp.concatenate([last_cell, last_cell], along),
        lax.slice_in_dim(padded, total_len - 2, total_len, axis=along),
    )
    return jnp.concatenate(
        [low_ghosts, lax.slice_in_dim(padded, 2, total_len - 2, axis=along), high_ghosts], along
    )


def face_edges(face_speed, comp, position, flag_open):
    n = face_speed.shape[comp]
    low_face = lax.slice_in_dim(face_speed, 0, 1, axis=comp) * jnp.where(
        position == 0, flag_open[2 * comp], 1.0
    )
    last_face = lax.slice_in_dim(face_speed, n - 1, n, axis=comp) * flag_open[2 * comp + 1]
    return (low_face, last_face)


def face_build(face_speed, comp, next_plane, position, count_on, flag_open):
    n = face_speed.shape[comp]
    low_face, last_face = face_edges(face_speed, comp, position, flag_open)
    high_face = jnp.where(
        position == count_on - 1, last_face, next_plane.astype(jnp.float32) / 256.0
    )
    face_rows = jnp.concatenate(
        [low_face, lax.slice_in_dim(face_speed, 1, n, axis=comp), high_face], comp
    )
    return face_rows[None]


def shards(density, momentum, energy, displacement, flags):
    fields = jnp.concatenate([density[None], momentum, energy[None]], 0)
    face_speed = displacement.astype(jnp.float32) / 256.0
    flag_open = flags.astype(jnp.float32)
    pos_x, pos_y, pos_z = (lax.axis_index("gx"), lax.axis_index("gy"), lax.axis_index("gz"))
    size_x, size_y, size_z = (lax.axis_size("gx"), lax.axis_size("gy"), lax.axis_size("gz"))
    cell_total = float(
        fields.shape[1] * fields.shape[2] * fields.shape[3] * size_x * size_y * size_z
    )
    next_xplane = from_behind(displacement[0, 0:1], "gx", -1)
    next_yplane = from_behind(displacement[1, :, 0:1], "gy", -1)
    next_zplane = from_behind(displacement[2, :, :, 0:1], "gz", -1)
    faces_x = face_build(face_speed[0], 0, next_xplane, pos_x, size_x, flag_open)
    faces_y = face_build(face_speed[1], 1, next_yplane, pos_y, size_y, flag_open)
    faces_z = face_build(face_speed[2], 2, next_zplane, pos_z, size_z, flag_open)
    along_x = padded_2(fields, (("gx", 1),), 2)
    along_y = padded_2(fields, (("gy", 2),), 2)
    along_z = padded_2(fields, (("gz", 3),), 2)
    updated = fields + flux_change(fix_ghosts(along_x, 1, pos_x, size_x), faces_x, 1)
    updated = updated + flux_change(fix_ghosts(along_y, 2, pos_y, size_y), faces_y, 2)
    updated = updated + flux_change(fix_ghosts(along_z, 3, pos_z, size_z), faces_z, 3)
    mass_sum, energy_sum = lax.psum((jnp.sum(updated[0]), jnp.sum(updated[4])), ("gx", "gy", "gz"))
    totals = jnp.stack([mass_sum, energy_sum]) / cell_total
    return (updated[0], updated[1:4], updated[4], totals)


def solution(mesh):
    return jax.shard_map(
        shards,
        mesh=mesh,
        in_specs=(
            P("gx", "gy", "gz"),
            P(None, "gx", "gy", "gz"),
            P("gx", "gy", "gz"),
            P(None, "gx", "gy", "gz"),
            P(),
        ),
        out_specs=(P("gx", "gy", "gz"), P(None, "gx", "gy", "gz"), P("gx", "gy", "gz"), P()),
        check_vma=False,
    )
```

profile of v0, /device:TPU:0, one launch (start us, length us, event | category | flops | bytes accessed | tf_op | source)
XLA Modules:
  0.0 120.2 jit_solution(10751196906076878649)
XLA Ops:
  0.6 1.4 %pad_maximum_fusion.15 = f32[5,8,64,128]{3,2,1,0:T(8,128)S(1)} fusion(f32[1,8,64,128]{3,2,1,0:T(8,128)} %bitcast.35, f32[3,8,64,128]{3,2,1,0:T(8,128)} %param.6, f32[1,8,64,128]{3,2,1,0:T(8,128)} %bitcast.43), kind=kLoop, calls=%fused_computation.45 | loop fusion | flops 655360 | bytes 2621440 | tf_op jit(solution)/shard_map/concatenate | solution.py:97
  2.0 1.6 %fusion.24 = (f32[5,8,64,2]{3,2,1,0:T(8,128)}, f32[5,8,64,2]{3,2,1,0:T(8,128)S(1)}) fusion(f32[5,8,64,128]{3,2,1,0:T(8,128)S(1)} %pad_maximum_fusion.15), kind=kLoop, calls=%fused_computation.91 | loop fusion | bytes 81920 | tf_op jit(solution)/shard_map/slice | solution.py:19
  3.5 2.4 %copy.143 = f32[5,8,64,2]{2,1,3,0:T(8,128)} copy(f32[5,8,64,2]{3,2,1,0:T(8,128)} %get-tuple-element.32) | data formatting | bytes 40960 | tf_op jit(solution)/shard_map/slice | solution.py:19
  6.0 3.0 %collective-permute-start.7 = (f32[5,8,64,2]{2,1,3,0:T(8,128)}, f32[5,8,64,2]{2,1,3,0:T(8,128)}, u32[]{:S(2)}, u32[]{:S(2)}) collective-permute-start(f32[5,8,64,2]{2,1,3,0:T(8,128)} %copy.143), channel_id=1, source_target_pairs={{0,1},{2,3},{4,5},{6,7},{8,9},{10,11},{12,13},{14,15},{16,17},{18,... | collective-permute-start | bytes 61448 | tf_op jit(solution)/shard_map/ppermute | solution.py:18
  9.0 1.1 copy.145
  10.0 1.3 %collective-permute-start.8 = (f32[5,8,64,2]{2,1,3,0:T(8,128)}, f32[5,8,64,2]{2,1,3,0:T(8,128)}, u32[]{:S(2)}, u32[]{:S(2)}) collective-permute-start(f32[5,8,64,2]{2,1,3,0:T(8,128)} %copy.145), channel_id=1, source_target_pairs={{1,0},{3,2},{5,4},{7,6},{9,8},{11,10},{13,12},{15,14},{17,16},{19,... | collective-permute-start | bytes 61448 | tf_op jit(solution)/shard_map/ppermute | solution.py:21
  11.5 0.9 copy.142
  12.4 1.3 %collective-permute-start.6 = (s32[8,64,1]{2,1,0:T(8,128)}, s32[8,64,1]{2,1,0:T(8,128)}, u32[]{:S(2)}, u32[]{:S(2)}) collective-permute-start(s32[8,64,1]{2,1,0:T(8,128)} %copy.142), channel_id=1, source_target_pairs={{1,0},{3,2},{5,4},{7,6},{9,8},{11,10},{13,12},{15,14},{17,16},{19,... | collective-permute-start | bytes 6152 | tf_op jit(solution)/shard_map/ppermute | solution.py:10
  13.7 0.6 copy.137
  14.3 4.9 %collective-permute-start.4 = (f32[5,8,2,128]{3,1,2,0:T(8,128)}, f32[5,8,2,128]{3,1,2,0:T(8,128)}, u32[]{:S(2)}, u32[]{:S(2)}) collective-permute-start(f32[5,8,2,128]{3,1,2,0:T(8,128)} %copy.137), channel_id=1, source_target_pairs={{0,2},{2,4},{4,6},{1,3},{3,5},{5,7},{8,10},{10,12},{12,14},{9,11},... | collective-permute-start | bytes 122888 | tf_op jit(solution)/shard_map/ppermute | solution.py:18
  19.2 0.6 copy.139
  19.8 1.3 %collective-permute-start.5 = (f32[5,8,2,128]{3,1,2,0:T(8,128)}, f32[5,8,2,128]{3,1,2,0:T(8,128)}, u32[]{:S(2)}, u32[]{:S(2)}) collective-permute-start(f32[5,8,2,128]{3,1,2,0:T(8,128)} %copy.139), channel_id=1, source_target_pairs={{2,0},{4,2},{6,4},{3,1},{5,3},{7,5},{10,8},{12,10},{14,12},{11,9},... | collective-permute-start | bytes 122888 | tf_op jit(solution)/shard_map/ppermute | solution.py:21
  21.1 2.0 %fusion.23 = (f32[5,8,64,1]{3,2,1,0:T(8,128)}, f32[5,8,64,1]{3,2,1,0:T(8,128)}) fusion(f32[5,8,64,128]{3,2,1,0:T(8,128)S(1)} %pad_maximum_fusion.15), kind=kLoop, calls=%fused_computation.90 | loop fusion | bytes 40960 | tf_op jit(solution)/shard_map/slice | solution.py:58
  23.2 0.7 fusion.22
  23.9 0.9 fusion.20
  24.8 0.8 fusion.19
  25.6 0.6 slice_bitcast_fusion.5
  26.3 0.7 fusion.25
  27.6 0.8 slice_bitcast_fusion.6
  29.9 1.3 %collective-permute-start.3 = (s32[8,1,128]{2,1,0:T(1,128)S(1)}, s32[8,1,128]{2,1,0:T(1,128)S(1)}, u32[]{:S(2)}, u32[]{:S(2)}) collective-permute-start(s32[8,1,128]{2,1,0:T(1,128)S(1)} %slice_bitcast_fusion.6), channel_id=1, source_target_pairs={{2,0},{4,2},{6,4},{3,1},{5,3},{7,5},{10,8},{12,10},{14,12},{11,9},... | collective-permute-start | bytes 12296 | tf_op jit(solution)/shard_map/ppermute | solution.py:10
  31.2 1.8 %slice_multiply_fusion.7 = (f32[8,64,1]{2,1,0:T(8,128)S(1)}, f32[8,64,1]{2,1,0:T(8,128)S(1)}) fusion(f32[8,64,128]{2,1,0:T(8,128)S(1)} %get-tuple-element.35, f32[]{:T(128)S(6)} %select_n.104, s32[8,64,1]{2,1,0:T(8,128)} %collective-permute-done.6, f32[]{:T(128)} %bitcast.15, pred[]{:T(512)S(6)} %eq.29), kind=kLoop, calls=%fused_computation.62 | loop fusion | flops 2560 | bytes 10249 | tf_op jit(solution)/shard_map/mul | solution.py:77
  33.2 1.1 subtract_multiply_fusion
  34.4 1.7 %collective-permute-done.3 = s32[8,1,128]{2,1,0:T(1,128)S(1)} collective-permute-done((s32[8,1,128]{2,1,0:T(1,128)S(1)}, s32[8,1,128]{2,1,0:T(1,128)S(1)}, u32[]{:S(2)}, u32[]{:S(2)}) %collective-permute-start.3) | collective-permute-done | bytes 4128 | tf_op jit(solution)/shard_map/ppermute | solution.py:10
  36.1 4.1 %collective-permute-start.1 = (f32[5,2,64,128]{3,2,1,0:T(8,128)}, f32[5,2,64,128]{3,2,1,0:T(8,128)}, u32[]{:S(2)}, u32[]{:S(2)}) collective-permute-start(f32[5,2,64,128]{3,2,1,0:T(8,128)} %get-tuple-element.24), channel_id=1, source_target_pairs={{0,8},{8,16},{16,24},{1,9},{9,17},{17,25},{2,10},{10,18},{18,26},{... | collective-permute-start | bytes 983048 | tf_op jit(solution)/shard_map/ppermute | solution.py:18
  40.7 1.0 pad_maximum_fusion.18
  41.8 0.7 broadcast_compare_fusion.1
  42.5 1.3 %collective-permute-start.2 = (f32[5,2,64,128]{3,2,1,0:T(8,128)}, f32[5,2,64,128]{3,2,1,0:T(8,128)}, u32[]{:S(2)}, u32[]{:S(2)}) collective-permute-start(f32[5,2,64,128]{3,2,1,0:T(8,128)} %get-tuple-element.25), channel_id=1, source_target_pairs={{8,0},{16,8},{24,16},{9,1},{17,9},{25,17},{10,2},{18,10},{26,18},{... | collective-permute-start | bytes 983048 | tf_op jit(solution)/shard_map/ppermute | solution.py:21
  43.8 2.3 %copy.146 = f32[5,8,64,2]{3,2,1,0:T(8,128)} copy(f32[5,8,64,2]{2,1,3,0:T(8,128)} %collective-permute-done.8) | data formatting | bytes 40960 | tf_op jit(solution)/shard_map/ppermute | solution.py:21
  46.1 2.6 %maximum_select_fusion.1 = f32[5,8,64,2]{3,2,1,0:T(8,128)S(1)} fusion(f32[5,8,64,2]{3,2,1,0:T(8,128)} %copy.146, f32[5,8,64,1]{3,2,1,0:T(8,128)} %get-tuple-element.31, pred[]{:T(512)S(6)} %eq.29), kind=kLoop, calls=%fused_computation.47 | loop fusion | flops 10240 | bytes 51201 | tf_op jit(solution)/shard_map/jit(_where)/select_n | solution.py:65
  48.8 1.7 %pad_maximum_fusion.4 = f32[5,8,64,130]{3,2,1,0:T(8,128)} fusion(f32[5,8,64,2]{3,2,1,0:T(8,128)S(1)} %maximum_select_fusion.1, f32[1,8,64,128]{3,2,1,0:T(8,128)S(1)} %bitcast.36, f32[3,8,64,128]{3,2,1,0:T(8,128)S(1)} %copy-done, f32[1,8,64,128]{3,2,1,0:T(8,128)S(1)} %bitcast.44), kind=kLoop, calls=%fused_computation.11 | loop fusion | flops 998400 | bytes 2662400 | tf_op jit(solution)/shard_map/concatenate | solution.py:70
  50.5 1.5 %collective-permute-start = (s32[1,64,128]{2,1,0:T(8,128)}, s32[1,64,128]{2,1,0:T(8,128)}, u32[]{:S(2)}, u32[]{:S(2)}) collective-permute-start(s32[1,64,128]{2,1,0:T(8,128)} %slice_bitcast_fusion.5), channel_id=1, source_target_pairs={{8,0},{16,8},{24,16},{9,1},{17,9},{25,17},{10,2},{18,10},{26,18},{... | collective-permute-start | bytes 98312 | tf_op jit(solution)/shard_map/ppermute | solution.py:10
  52.0 2.4 %copy.144 = f32[5,8,64,2]{3,2,1,0:T(8,128)} copy(f32[5,8,64,2]{2,1,3,0:T(8,128)} %collective-permute-done.7) | data formatting | bytes 40960 | tf_op jit(solution)/shard_map/ppermute | solution.py:18
  54.3 2.1 %maximum_select_fusion = f32[5,8,64,2]{3,2,1,0:T(8,128)S(1)} fusion(f32[5,8,64,2]{3,2,1,0:T(8,128)} %copy.144, f32[5,8,64,1]{3,2,1,0:T(8,128)} %get-tuple-element.30, pred[]{:T(512)S(6)} %eq.28), kind=kLoop, calls=%fused_computation.46 | loop fusion | flops 10240 | bytes 51201 | tf_op jit(solution)/shard_map/jit(_where)/select_n | solution.py:60
  56.5 3.1 %maximum_maximum_fusion = (f32[5,8,64,130]{3,2,1,0:T(8,128)S(1)}, f32[5,8,64,130]{3,2,1,0:T(8,128)S(1)}) fusion(f32[1,8,64,128]{3,2,1,0:T(8,128)S(1)} %bitcast.37, f32[3,8,64,128]{3,2,1,0:T(8,128)S(1)} %copy-done, f32[1,8,64,128]{3,2,1,0:T(8,128)S(1)} %bitcast.45, f32[5,8,64,2]{3,2,1,0:T(8,128)S(1)} %maximum_select_fusion, ...), kind=kLoop, calls=%fused_computation.10 | loop fusion | flops 6656000 | bytes 4014080 | tf_op jit(solution)/shard_map/concatenate | solution.py:70
  59.6 1.4 %fusion.2 = f32[5,8,64,129]{3,2,1,0:T(8,128)S(1)} fusion(f32[5,8,64,130]{3,2,1,0:T(8,128)S(1)} %get-tuple-element.15, f32[5,8,64,130]{3,2,1,0:T(8,128)S(1)} %copy-done.3, f32[5,8,64,130]{3,2,1,0:T(8,128)S(1)} %get-tuple-element.14, f32[8,64,129]{2,1,0:T(8,128)S(1)} %copy-done.6, f32[8,64,129]{2,1,0:T(8,128)S(1)} %copy-done.5, ...), kind=kLoop, calls=%fused_computation.3 | loop fusion | flops 1981440 | bytes 7463424 | tf_op jit(solution)/shard_map/mul | solution.py:45
  61.1 1.5 %fusion.17 = f32[1,64,128]{2,1,0:T(8,128)S(1)} fusion(f32[3,8,64,128]{3,2,1,0:T(8,128)} %copy-done.4, s32[1,64,128]{2,1,0:T(8,128)} %collective-permute-done, f32[]{:T(128)} %bitcast.5, pred[]{:T(512)S(6)} %eq.25), kind=kLoop, calls=%fused_computation.77 | loop fusion | flops 32768 | bytes 98309 | tf_op jit(solution)/shard_map/jit(_where)/select_n | solution.py:87
  62.7 0.8 maximum_select_fusion.5
  63.7 0.8 maximum_select_fusion.4
  64.6 1.3 %maximum_maximum_fusion.2 = (f32[5,8,66,128]{3,2,1,0:T(8,128)S(1)}, f32[5,8,66,128]{3,2,1,0:T(8,128)S(1)}) fusion(f32[1,8,64,128]{3,2,1,0:T(8,128)S(1)} %bitcast.39, f32[3,8,64,128]{3,2,1,0:T(8,128)S(1)} %copy-done, f32[1,8,64,128]{3,2,1,0:T(8,128)S(1)} %bitcast.47, f32[5,8,2,128]{3,2,1,0:T(2,128)S(1)} %maximum_select_fusion.4, ...), kind=kLoop, calls=%fused_computation.36 | loop fusion | flops 6758400 | bytes 4096000 | tf_op jit(solution)/shard_map/concatenate | solution.py:70
  66.8 1.0 maximum_select_fusion.3
  68.0 0.8 copy-done.11
  68.8 1.2 %maximum_maximum_fusion.1 = (f32[5,10,64,128]{3,2,1,0:T(8,128)S(1)}, f32[5,10,64,128]{3,2,1,0:T(8,128)S(1)}) fusion(f32[1,8,64,128]{3,2,1,0:T(8,128)S(1)} %bitcast.41, f32[3,8,64,128]{3,2,1,0:T(8,128)S(1)} %copy-done, f32[1,8,64,128]{3,2,1,0:T(8,128)S(1)} %bitcast.49, f32[5,2,64,128]{3,2,1,0:T(8,128)S(1)} %maximum_select_fusion.2, ...), kind=kLoop, calls=%fused_computation.17 | loop fusion | flops 8192000 | bytes 5242880 | tf_op jit(solution)/shard_map/concatenate | solution.py:70
  70.0 0.6 fusion.10
  70.7 0.8 fusion.12
  71.4 1.5 %slice_reduce_fusion.1 = (f32[]{:T(128)}, f32[]{:T(128)}, f32[8,64,128]{2,1,0:T(8,128)}, f32[8,64,128]{2,1,0:T(8,128)}) fusion(f32[5,8,64,128]{3,2,1,0:T(8,128)S(1)} %fusion.12), kind=kLoop, calls=%fused_computation.68 | loop fusion | flops 131070 | bytes 1048584 | tf_op jit(solution)/shard_map/reduce_sum | solution.py:117
  72.9 0.9 slice.302
  73.9 44.5 %all-reduce = (f32[1]{0:T(128)}, f32[1]{0:T(128)}) all-reduce(f32[1]{0:T(128)} %bitcast.20, f32[1]{0:T(128)} %bitcast.19), channel_id=1, replica_groups=mesh['gx'=4,'gy'=4,'gz'=2] {'gx','gy','gz'}, use_global_device_ids=true, to_apply=%region_3.4 | all-reduce | flops 2 | bytes 16 | tf_op jit(solution)/shard_map/psum | solution.py:117
  118.4 1.8 %maximum_multiply_fusion = f32[2]{0:T(128)} fusion(f32[1]{0:T(128)} %get-tuple-element.10, f32[1]{0:T(128)} %get-tuple-element.11), kind=kLoop, calls=%fused_computation.85 | loop fusion | flops 4 | bytes 16 | tf_op jit(solution)/shard_map/div | solution.py:118
  (59 shorter events, 2.6 us)
Async XLA Ops:
  3.5 7.8 %copy-start.7 = (s32[3,8,64,128]{3,2,1,0:T(8,128)S(1)}, s32[3,8,64,128]{3,2,1,0:T(8,128)}, u32[]{:S(2)}) copy-start(s32[3,8,64,128]{3,2,1,0:T(8,128)} %param.8) | copy-start | bytes 2359300
  6.0 44.5 %collective-permute-start.7 = (f32[5,8,64,2]{2,1,3,0:T(8,128)}, f32[5,8,64,2]{2,1,3,0:T(8,128)}, u32[]{:S(2)}, u32[]{:S(2)}) collective-permute-start(f32[5,8,64,2]{2,1,3,0:T(8,128)} %copy.143), channel_id=1, source_target_pairs={{0,1},{2,3},{4,5},{6,7},{8,9},{10,11},{12,13},{14,15},{16,17},{18,... | collective-permute-start | bytes 61448 | tf_op jit(solution)/shard_map/ppermute | solution.py:18
  10.0 32.5 %collective-permute-start.8 = (f32[5,8,64,2]{2,1,3,0:T(8,128)}, f32[5,8,64,2]{2,1,3,0:T(8,128)}, u32[]{:S(2)}, u32[]{:S(2)}) collective-permute-start(f32[5,8,64,2]{2,1,3,0:T(8,128)} %copy.145), channel_id=1, source_target_pairs={{1,0},{3,2},{5,4},{7,6},{9,8},{11,10},{13,12},{15,14},{17,16},{19,... | collective-permute-start | bytes 61448 | tf_op jit(solution)/shard_map/ppermute | solution.py:21
  12.4 17.6 %collective-permute-start.6 = (s32[8,64,1]{2,1,0:T(8,128)}, s32[8,64,1]{2,1,0:T(8,128)}, u32[]{:S(2)}, u32[]{:S(2)}) collective-permute-start(s32[8,64,1]{2,1,0:T(8,128)} %copy.142), channel_id=1, source_target_pairs={{1,0},{3,2},{5,4},{7,6},{9,8},{11,10},{13,12},{15,14},{17,16},{19,... | collective-permute-start | bytes 6152 | tf_op jit(solution)/shard_map/ppermute | solution.py:10
  14.3 49.3 %collective-permute-start.4 = (f32[5,8,2,128]{3,1,2,0:T(8,128)}, f32[5,8,2,128]{3,1,2,0:T(8,128)}, u32[]{:S(2)}, u32[]{:S(2)}) collective-permute-start(f32[5,8,2,128]{3,1,2,0:T(8,128)} %copy.137), channel_id=1, source_target_pairs={{0,2},{2,4},{4,6},{1,3},{3,5},{5,7},{8,10},{10,12},{12,14},{9,11},... | collective-permute-start | bytes 122888 | tf_op jit(solution)/shard_map/ppermute | solution.py:18
  19.8 42.8 %collective-permute-start.5 = (f32[5,8,2,128]{3,1,2,0:T(8,128)}, f32[5,8,2,128]{3,1,2,0:T(8,128)}, u32[]{:S(2)}, u32[]{:S(2)}) collective-permute-start(f32[5,8,2,128]{3,1,2,0:T(8,128)} %copy.139), channel_id=1, source_target_pairs={{2,0},{4,2},{6,4},{3,1},{5,3},{7,5},{10,8},{12,10},{14,12},{11,9},... | collective-permute-start | bytes 122888 | tf_op jit(solution)/shard_map/ppermute | solution.py:21
  23.2 4.4 %copy-start.4 = (f32[3,8,64,128]{3,2,1,0:T(8,128)}, f32[3,8,64,128]{3,2,1,0:T(8,128)S(1)}, u32[]{:S(2)}) copy-start(f32[3,8,64,128]{3,2,1,0:T(8,128)S(1)} %convert_multiply_fusion) | copy-start | bytes 2359300
  23.9 2.3 %copy-start.16 = (s32[6]{0:T(128)S(1)}, s32[6]{0:T(128)}, u32[]{:S(2)}) copy-start(s32[6]{0:T(128)} %param.9) | copy-start | bytes 76
  29.9 6.1 %collective-permute-start.3 = (s32[8,1,128]{2,1,0:T(1,128)S(1)}, s32[8,1,128]{2,1,0:T(1,128)S(1)}, u32[]{:S(2)}, u32[]{:S(2)}) collective-permute-start(s32[8,1,128]{2,1,0:T(1,128)S(1)} %slice_bitcast_fusion.6), channel_id=1, source_target_pairs={{2,0},{4,2},{6,4},{3,1},{5,3},{7,5},{10,8},{12,10},{14,12},{11,9},... | collective-permute-start | bytes 12296 | tf_op jit(solution)/shard_map/ppermute | solution.py:10
  36.1 31.9 %collective-permute-start.1 = (f32[5,2,64,128]{3,2,1,0:T(8,128)}, f32[5,2,64,128]{3,2,1,0:T(8,128)}, u32[]{:S(2)}, u32[]{:S(2)}) collective-permute-start(f32[5,2,64,128]{3,2,1,0:T(8,128)} %get-tuple-element.24), channel_id=1, source_target_pairs={{0,8},{8,16},{16,24},{1,9},{9,17},{17,25},{2,10},{10,18},{18,26},{... | collective-permute-start | bytes 983048 | tf_op jit(solution)/shard_map/ppermute | solution.py:18
  42.5 23.9 %collective-permute-start.2 = (f32[5,2,64,128]{3,2,1,0:T(8,128)}, f32[5,2,64,128]{3,2,1,0:T(8,128)}, u32[]{:S(2)}, u32[]{:S(2)}) collective-permute-start(f32[5,2,64,128]{3,2,1,0:T(8,128)} %get-tuple-element.25), channel_id=1, source_target_pairs={{8,0},{16,8},{24,16},{9,1},{17,9},{25,17},{10,2},{18,10},{26,18},{... | collective-permute-start | bytes 983048 | tf_op jit(solution)/shard_map/ppermute | solution.py:21
  46.1 2.6 %copy-start = (f32[3,8,64,128]{3,2,1,0:T(8,128)S(1)}, f32[3,8,64,128]{3,2,1,0:T(8,128)}, u32[]{:S(2)}) copy-start(f32[3,8,64,128]{3,2,1,0:T(8,128)} %param.6) | copy-start | bytes 2359300
  46.1 2.6 %copy-start.1 = (f32[8,64,128]{2,1,0:T(8,128)S(1)}, f32[8,64,128]{2,1,0:T(8,128)}, u32[]{:S(2)}) copy-start(f32[8,64,128]{2,1,0:T(8,128)} %param.7) | copy-start | bytes 786436
  46.1 2.6 %copy-start.2 = (f32[8,64,128]{2,1,0:T(8,128)S(1)}, f32[8,64,128]{2,1,0:T(8,128)}, u32[]{:S(2)}) copy-start(f32[8,64,128]{2,1,0:T(8,128)} %param.5) | copy-start | bytes 786436
  50.5 10.6 %collective-permute-start = (s32[1,64,128]{2,1,0:T(8,128)}, s32[1,64,128]{2,1,0:T(8,128)}, u32[]{:S(2)}, u32[]{:S(2)}) collective-permute-start(s32[1,64,128]{2,1,0:T(8,128)} %slice_bitcast_fusion.5), channel_id=1, source_target_pairs={{8,0},{16,8},{24,16},{9,1},{17,9},{25,17},{10,2},{18,10},{26,18},{... | collective-permute-start | bytes 98312 | tf_op jit(solution)/shard_map/ppermute | solution.py:10
  56.5 3.1 %copy-start.3 = (f32[5,8,64,130]{3,2,1,0:T(8,128)S(1)}, f32[5,8,64,130]{3,2,1,0:T(8,128)}, u32[]{:S(2)}) copy-start(f32[5,8,64,130]{3,2,1,0:T(8,128)} %pad_maximum_fusion.4) | copy-start | bytes 3993604
  56.5 3.1 %copy-start.5 = (f32[8,64,129]{2,1,0:T(8,128)S(1)}, f32[8,64,129]{2,1,0:T(8,128)}, u32[]{:S(2)}) copy-start(f32[8,64,129]{2,1,0:T(8,128)} %get-tuple-element.36) | copy-start | bytes 792580
  56.5 3.1 %copy-start.6 = (f32[8,64,129]{2,1,0:T(8,128)S(1)}, f32[8,64,129]{2,1,0:T(8,128)}, u32[]{:S(2)}) copy-start(f32[8,64,129]{2,1,0:T(8,128)} %get-tuple-element.37) | copy-start | bytes 792580
  61.1 1.6 %copy-start.15 = (f32[5,8,1,128]{3,2,1,0:T(1,128)S(1)}, f32[5,8,1,128]{3,2,1,0:T(1,128)}, u32[]{:S(2)}) copy-start(f32[5,8,1,128]{3,2,1,0:T(1,128)} %get-tuple-element.29) | copy-start | bytes 61444
  62.7 1.0 copy-start.14
  64.5 1.3 %copy-start.8 = (f32[8,65,128]{2,1,0:T(8,128)S(1)}, f32[8,65,128]{2,1,0:T(8,128)}, u32[]{:S(2)}) copy-start(f32[8,65,128]{2,1,0:T(8,128)} %get-tuple-element.41) | copy-start | bytes 798724
  64.5 1.3 %copy-start.9 = (f32[8,65,128]{2,1,0:T(8,128)S(1)}, f32[8,65,128]{2,1,0:T(8,128)}, u32[]{:S(2)}) copy-start(f32[8,65,128]{2,1,0:T(8,128)} %get-tuple-element.42) | copy-start | bytes 798724
  64.5 1.3 %copy-start.10 = (f32[8,65,128]{2,1,0:T(8,128)S(1)}, f32[8,65,128]{2,1,0:T(8,128)}, u32[]{:S(2)}) copy-start(f32[8,65,128]{2,1,0:T(8,128)} %get-tuple-element.43) | copy-start | bytes 798724
  64.5 1.3 %copy-start.13 = (pred[8,65,128]{2,1,0:T(8,128)(4,1)S(1)}, pred[8,65,128]{2,1,0:T(8,128)(4,1)}, u32[]{:S(2)}) copy-start(pred[8,65,128]{2,1,0:T(8,128)(4,1)} %broadcast_compare_fusion.1) | copy-start | bytes 199684
  65.9 0.9 copy-start.12
  67.8 0.9 copy-start.11
where the time goes:
time: 121 us; the launch traced here: 120 us
  blocking collectives  44.5 us (37%)
  other arithmetic  30.2 us (25%)
  local copies, waits for them, and re-layouts  20.8 us (17%)
  starting transfers between devices  19.9 us (16%)
  between operations  3.16 us (3%)
  waiting for transfers between devices  1.73 us (1%)
    psum x1, blocking collectives, shards(): lax.psum((jnp.sum(updated[0]), jnp.sum(updated[4])), ('gx', 'gy', 'gz'))  44.5 us
    ppermute x3, starting transfers between devices, padded_2(): lax.ppermute(lax.slice_in_dim(block, block.shape[dim] - width, None, axis...  12 us
    concatenate x6, other arithmetic, fix_ghosts(): jnp.concatenate([low_ghosts, lax.slice_in_dim(padded, 2, total_len - 2, a...  7.61 us
    slice x5, local copies, waits for them, and re-layouts, padded_2(): lax.slice_in_dim(block, block.shape[dim] - width, None, axis=dim)  5.54 us
    select_n x3, other arithmetic, fix_ghosts(): jnp.where(position == count_on - 1, jnp.concatenate([last_cell, last_cell...  4.44 us
    ppermute x3, starting transfers between devices, from_behind(): lax.ppermute(value, axis, [(source, source + steps) for source in range(l...  4.03 us
    ppermute x3, starting transfers between devices, padded_2(): lax.ppermute(lax.slice_in_dim(block, 0, width, axis=dim), axis, backward)  3.84 us
    slice x3, local copies, waits for them, and re-layouts, fix_ghosts(): first_cell = lax.slice_in_dim(padded, 2, 3, axis=along)  3.47 us
  transfers between devices with their start and end apart: 9, of which 1 were waited for; matrix products, arithmetic and copies ran while one was open for 31% of the time, Pallas kernels for 0%

commit v1 on v0

v1 whole, which is shorter than its diff:
```python
import functools

import jax
import jax.numpy as jnp
from jax import lax
from jax.experimental import pallas as pl
from jax.experimental.pallas import tpu as pltpu
from jax.sharding import PartitionSpec as P

AXES = ("gx", "gy", "gz")
SUB = 8


def minmod(p, r):
    return jnp.maximum(jnp.minimum(r, 0.0), jnp.minimum(p, jnp.maximum(r, 0.0)))


def gain(v):
    size = jnp.abs(v)
    return 0.5 * size * (1.0 - size)


def flux(v, g, q_low, q_high, s_low, s_high):
    up = v > 0
    return v * jnp.where(up, q_low, q_high) + g * jnp.where(up, s_low, s_high)


def kernel(
    sizes, flags, den, mom, en, disp, out_d, out_m, out_e, totals,
    q, dx, dy, dz, xlo, xhi, xv, edge, zlo, zhi, cq, cs, sum_x, sum_y, sum_z,
    local_sem, send_sem, recv_sem, ssx, rsx, ssy, rsy, ssz, rsz,
):
    nx, ny, nz = den.shape
    pos = {a: lax.axis_index(a) for a in AXES}
    top = ny + SUB
    per = nz // 4
    parts = edge.shape[0]
    scale = 1.0 / 256.0
    cells = float(nx * ny * nz)
    for a in AXES:
        cells = cells * sizes[a]

    locals_ = [
        pltpu.make_async_copy(den, q.at[0, :, SUB:top], local_sem.at[0]),
        pltpu.make_async_copy(mom, q.at[1:4, :, SUB:top], local_sem.at[1]),
        pltpu.make_async_copy(en, q.at[4, :, SUB:top], local_sem.at[2]),
        pltpu.make_async_copy(disp.at[2], dz, local_sem.at[3]),
        pltpu.make_async_copy(disp.at[1], dy.at[:, SUB:top], local_sem.at[4]),
        pltpu.make_async_copy(disp.at[0], dx, local_sem.at[5]),
    ]
    for c in locals_:
        c.start()

    barrier = pltpu.get_barrier_semaphore()
    greeted = 0
    for a in AXES:
        for o in range(1, sizes[a]):
            peer = lax.rem(pos[a] + o, sizes[a])
            pl.semaphore_signal(
                barrier, inc=1, device_id={a: peer}, device_id_type=pl.DeviceIdType.MESH
            )
            greeted += 1
    pl.semaphore_wait(barrier, greeted)

    def copy(k, src, dst, axis, step):
        return pltpu.make_async_remote_copy(
            src_ref=src, dst_ref=dst, send_sem=send_sem.at[k], recv_sem=recv_sem.at[k],
            device_id={axis: pos[axis] + step}, device_id_type=pl.DeviceIdType.MESH,
        )

    last = {a: sizes[a] - 1 for a in AXES}
    x_up = [
        copy(0, den.at[nx - 2 : nx], xlo.at[0], "gx", 1),
        copy(1, mom.at[:, nx - 2 : nx], xlo.at[1:4], "gx", 1),
        copy(2, en.at[nx - 2 : nx], xlo.at[4], "gx", 1),
    ]
    x_down = [
        copy(3, den.at[0:2], xhi.at[0], "gx", -1),
        copy(4, mom.at[:, 0:2], xhi.at[1:4], "gx", -1),
        copy(5, en.at[0:2], xhi.at[4], "gx", -1),
        copy(6, disp.at[0, 0], xv, "gx", -1),
    ]
    hi_rows = slice(top, top + SUB)
    y_up = [
        copy(7, den.at[:, ny - SUB : ny], q.at[0, :, 0:SUB], "gy", 1),
        copy(8, mom.at[:, :, ny - SUB : ny], q.at[1:4, :, 0:SUB], "gy", 1),
        copy(9, en.at[:, ny - SUB : ny], q.at[4, :, 0:SUB], "gy", 1),
    ]
    y_down = [
        copy(10, den.at[:, 0:SUB], q.at[0, :, hi_rows], "gy", -1),
        copy(11, mom.at[:, :, 0:SUB], q.at[1:4, :, hi_rows], "gy", -1),
        copy(12, en.at[:, 0:SUB], q.at[4, :, hi_rows], "gy", -1),
        copy(13, disp.at[1, :, 0:SUB], dy.at[:, hi_rows], "gy", -1),
    ]
    z_up = [copy(14, edge, zlo, "gz", 1)]
    z_down = [copy(15, edge, zhi, "gz", -1)]

    def start(axis, ups, downs):
        @pl.when(pos[axis] < last[axis])
        def _():
            for c in ups:
                c.start()

        @pl.when(pos[axis] > 0)
        def _():
            for c in downs:
                c.start()

    def arrive(axis, ups, downs, fill_low, fill_high):
        @pl.when(pos[axis] > 0)
        def _():
            for c in ups:
                c.wait_recv()

        @pl.when(pos[axis] < last[axis])
        def _():
            for c in downs:
                c.wait_recv()

        @pl.when(pos[axis] == 0)
        def _():
            fill_low()

        @pl.when(pos[axis] == last[axis])
        def _():
            fill_high()

    def sent(axis, ups, downs):
        @pl.when(pos[axis] < last[axis])
        def _():
            for c in ups:
                c.wait_send()

        @pl.when(pos[axis] > 0)
        def _():
            for c in downs:
                c.wait_send()

    start("gx", x_up, x_down)
    start("gy", y_up, y_down)

    flag = [flags[i].astype(jnp.float32) for i in range(6)]

    def low_mult(a):
        return jnp.where(pos[AXES[a]] == 0, flag[2 * a], 1.0)

    def high_mult(a):
        return jnp.where(pos[AXES[a]] == last[AXES[a]], flag[2 * a + 1], 1.0)

    def outer_low(a):
        return jnp.where(pos[AXES[a]] == 0, flag[2 * a], 0.0)

    def outer_high(a):
        return jnp.where(pos[AXES[a]] == last[AXES[a]], flag[2 * a + 1], 0.0)

    for c in locals_:
        c.wait()

    lane = lax.broadcasted_iota(jnp.int32, (ny, nz), 1)
    row = lax.broadcasted_iota(jnp.int32, (ny, nz), 0)

    def pack(x, carry):
        new = list(carry)
        for f in range(6):
            p = f * nx + x
            k = f * nx // per
            at = 4 * lax.rem(p, per)
            plane = q[f, x, SUB:top] if f < 5 else dz[x].astype(jnp.float32)
            moved = pltpu.roll(plane, at, 1)
            mine = lax.rem(lane + 2 - at + nz, nz) < 4
            new[k] = jnp.where(mine, moved, new[k])
        return tuple(new)

    packed = lax.fori_loop(0, nx, pack, tuple(jnp.zeros((ny, nz), jnp.float32) for _ in range(parts)))
    for k in range(parts):
        edge[k] = packed[k]

    wz = jnp.where(lane == 0, outer_low(2), 0.0) - jnp.where(lane == nz - 1, outer_high(2), 0.0)
    wy = jnp.where(row == 0, outer_low(1), 0.0) - jnp.where(row == ny - 1, outer_high(1), 0.0)
    wx_low, wx_high = outer_low(0), outer_high(0)

    def total(x, carry):
        a, b = carry
        wx = jnp.where(x == 0, wx_low, 0.0) - jnp.where(x == nx - 1, wx_high, 0.0)
        w = 1.0 + scale * (
            wz * dz[x].astype(jnp.float32)
            + wy * dy[x, SUB:top].astype(jnp.float32)
            + wx * dx[x].astype(jnp.float32)
        )
        return (
            a + jnp.sum((q[0, x, SUB:top] * w).reshape(ny // SUB, SUB, nz), 0),
            b + jnp.sum((q[4, x, SUB:top] * w).reshape(ny // SUB, SUB, nz), 0),
        )

    zero = jnp.zeros((SUB, nz), jnp.float32)
    mass, power = lax.fori_loop(0, nx, total, (zero, zero))
    sum_z[pos["gz"], 0] = mass
    sum_z[pos["gz"], 1] = power
    start("gz", z_up, z_down)

    def line(axis, slots, ss, rs):
        count = sizes[axis]
        copies = []
        for o in range(1, count):
            me = pos[axis]
            copies.append(
                pltpu.make_async_remote_copy(
                    src_ref=slots.at[me], dst_ref=slots.at[me], send_sem=ss.at[o],
                    recv_sem=rs.at[me], device_id={axis: lax.rem(me + o, count)},
                    device_id_type=pl.DeviceIdType.MESH,
                )
            )
        return copies

    def collect(axis, slots, ss, rs):
        count = sizes[axis]
        for o in range(1, count):
            peer = lax.rem(pos[axis] + o, count)
            pltpu.make_async_remote_copy(
                src_ref=slots.at[peer], dst_ref=slots.at[peer], send_sem=ss.at[o],
                recv_sem=rs.at[peer], device_id={axis: peer},
                device_id_type=pl.DeviceIdType.MESH,
            ).wait_recv()
        a, b = slots[0, 0], slots[0, 1]
        for o in range(1, count):
            a = a + slots[o, 0]
            b = b + slots[o, 1]
        return a, b

    line_z = line("gz", sum_z, ssz, rsz)
    line_y = line("gy", sum_y, ssy, rsy)
    line_x = line("gx", sum_x, ssx, rsx)
    for c in line_z:
        c.start()

    def z_low():
        e = edge[...]
        zlo[...] = jnp.where(lane3 & 3 == 3, pltpu.roll(e, nz - 1, 2), pltpu.roll(e, nz - 2, 2))

    def z_high():
        e = edge[...]
        zhi[...] = jnp.where(lane3 & 3 == 0, pltpu.roll(e, 1, 2), pltpu.roll(e, 2, 2))

    lane3 = lax.broadcasted_iota(jnp.int32, (parts, ny, nz), 2)
    arrive("gz", z_up, z_down, z_low, z_high)
    low = lane & 3 == 0
    for k in range(parts):
        e, l, h = edge[k], zlo[k], zhi[k]
        r1, r2 = pltpu.roll(l, 1, 1), pltpu.roll(l, 2, 1)
        l1, l2 = pltpu.roll(h, nz - 1, 1), pltpu.roll(h, nz - 2, 1)
        cq[k] = jnp.where(low, r1, l1)
        cs[k] = jnp.where(low, minmod(e - r1, r1 - r2), minmod(l2 - l1, l1 - e))

    first, final = lane == 0, lane == nz - 1
    z_lo_mult = jnp.where(first, low_mult(2), 1.0) * scale
    z_hi_mult = high_mult(2) * scale
    outs = (
        lambda x: out_d.at[x], lambda x: out_m.at[0, x], lambda x: out_m.at[1, x],
        lambda x: out_m.at[2, x], lambda x: out_e.at[x],
    )

    def along_z(x, _):
        v = dz[x].astype(jnp.float32) * z_lo_mult
        g = gain(v)

        def ghosts(ref, f):
            back = lax.rem(nz - 4 * lax.rem(f * nx + x, per), nz)
            return pltpu.roll(ref[f * nx // per], back, 1)

        vh = ghosts(cq, 5) * z_hi_mult
        gh = gain(vh)
        for f in range(5):
            plane = q[f, x, SUB:top]
            gq, gs = ghosts(cq, f), ghosts(cs, f)
            qm = jnp.where(first, gq, pltpu.roll(plane, 1, 1))
            d = plane - qm
            s = minmod(jnp.where(final, gq - plane, pltpu.roll(d, nz - 1, 1)), d)
            sm = jnp.where(first, gs, pltpu.roll(s, 1, 1))
            fl = flux(v, g, qm, plane, sm, s)
            fh = jnp.where(final, flux(vh, gh, plane, gq, s, gs), pltpu.roll(fl, nz - 1, 1))
            outs[f](x)[...] = plane + (fl - fh)
        return 0

    lax.fori_loop(0, nx, along_z, 0)

    a, b = collect("gz", sum_z, ssz, rsz)
    sum_y[pos["gy"], 0] = a
    sum_y[pos["gy"], 1] = b

    def y_low():
        q[:, :, 0:SUB] = jnp.broadcast_to(q[:, :, SUB : SUB + 1], (5, nx, SUB, nz))

    def y_high():
        q[:, :, hi_rows] = jnp.broadcast_to(q[:, :, top - 1 : top], (5, nx, SUB, nz))
        dy[:, hi_rows] = jnp.broadcast_to(dy[:, top - 1 : top], (nx, SUB, nz))

    arrive("gy", y_up, y_down, y_low, y_high)
    for c in line_y:
        c.start()
    tall = ny + 2 * SUB
    rows = lax.broadcasted_iota(jnp.int32, (tall, nz), 0)
    inside = (rows >= SUB) & (rows <= top)
    y_mult = jnp.where(
        rows == SUB, low_mult(1) * scale, jnp.where(rows == top, high_mult(1) * scale, scale)
    )

    def along_y(x, _):
        v = jnp.where(inside, dy[x].astype(jnp.float32), 0.0) * y_mult
        g = gain(v)
        for f in range(5):
            plane = q[f, x]
            qm = pltpu.roll(plane, 1, 0)
            d = plane - qm
            s = minmod(pltpu.roll(d, tall - 1, 0), d)
            fl = flux(v, g, qm, plane, pltpu.roll(s, 1, 0), s)
            ch = fl - pltpu.roll(fl, tall - 1, 0)
            outs[f](x)[...] += ch[SUB:top]
        return 0

    lax.fori_loop(0, nx, along_y, 0)

    a, b = collect("gy", sum_y, ssy, rsy)
    sum_x[pos["gx"], 0] = a
    sum_x[pos["gx"], 1] = b

    def x_low():
        xlo[...] = jnp.broadcast_to(q[:, 0:1, SUB:top], (5, 2, ny, nz))

    def x_high():
        xhi[...] = jnp.broadcast_to(q[:, nx - 1 : nx, SUB:top], (5, 2, ny, nz))
        xv[...] = dx[nx - 1]

    for c in line_x:
        c.start()
    arrive("gx", x_up, x_down, x_low, x_high)
    x_lo_mult, x_hi_mult = low_mult(0) * scale, high_mult(0) * scale

    def along_x(r, _):
        at = pl.ds(pl.multiple_of(r * SUB, SUB), SUB)
        inner = pl.ds(pl.multiple_of(r * SUB + SUB, SUB), SUB)
        vs = [dx[c, at].astype(jnp.float32) * (x_lo_mult if c == 0 else scale) for c in range(nx)]
        vs.append(xv[at].astype(jnp.float32) * x_hi_mult)
        gs = [gain(v) for v in vs]
        for f in range(5):
            line_q = (
                [xlo[f, 0, at], xlo[f, 1, at]]
                + [q[f, c, inner] for c in range(nx)]
                + [xhi[f, 0, at], xhi[f, 1, at]]
            )
            ds = [line_q[i + 1] - line_q[i] for i in range(nx + 3)]
            ss = [minmod(ds[i + 1], ds[i]) for i in range(nx + 2)]
            fl = [
                flux(vs[i], gs[i], line_q[i + 1], line_q[i + 2], ss[i], ss[i + 1])
                for i in range(nx + 1)
            ]
            for c in range(nx):
                ref = outs[f](c)
                ref[at] += fl[c] - fl[c + 1]
        return 0

    lax.fori_loop(0, ny // SUB, along_x, 0)

    a, b = collect("gx", sum_x, ssx, rsx)
    totals[0] = jnp.sum(a) / cells
    totals[1] = jnp.sum(b) / cells
    sent("gx", x_up, x_down)
    sent("gy", y_up, y_down)
    sent("gz", z_up, z_down)
    for c in line_x + line_y + line_z:
        c.wait_send()


def shards(density, momentum, energy, displacement, flags):
    sizes = {a: lax.axis_size(a) for a in AXES}
    nx, ny, nz = density.shape
    tall = ny + 2 * SUB
    per = nz // 4
    parts = -(-6 * nx // per)
    f32, i32 = jnp.float32, jnp.int32
    dma = pltpu.SemaphoreType.DMA
    any_ = pl.BlockSpec(memory_space=pl.ANY)
    vmem = pl.BlockSpec(memory_space=pltpu.VMEM)
    smem = pl.BlockSpec(memory_space=pltpu.SMEM)
    return pl.pallas_call(
        functools.partial(kernel, sizes),
        out_shape=(
            jax.ShapeDtypeStruct(density.shape, f32),
            jax.ShapeDtypeStruct(momentum.shape, f32),
            jax.ShapeDtypeStruct(energy.shape, f32),
            jax.ShapeDtypeStruct((2,), f32),
        ),
        in_specs=[smem, any_, any_, any_, any_],
        out_specs=(vmem, vmem, vmem, smem),
        scratch_shapes=[
            pltpu.VMEM((5, nx, tall, nz), f32),
            pltpu.VMEM((nx, ny, nz), i32),
            pltpu.VMEM((nx, tall, nz), i32),
            pltpu.VMEM((nx, ny, nz), i32),
            pltpu.VMEM((5, 2, ny, nz), f32),
            pltpu.VMEM((5, 2, ny, nz), f32),
            pltpu.VMEM((ny, nz), i32),
        ]
        + [pltpu.VMEM((parts, ny, nz), f32) for _ in range(5)]
        + [pltpu.VMEM((sizes[a], 2, SUB, nz), f32) for a in AXES]
        + [dma((6,)), dma((16,)), dma((16,))]
        + [dma((sizes[a],)) for a in AXES for _ in range(2)],
        compiler_params=pltpu.CompilerParams(collective_id=0, has_side_effects=True),
    )(flags, density, momentum, energy, displacement)


def solution(mesh):
    return jax.shard_map(
        shards,
        mesh=mesh,
        in_specs=(
            P("gx", "gy", "gz"),
            P(None, "gx", "gy", "gz"),
            P("gx", "gy", "gz"),
            P(None, "gx", "gy", "gz"),
            P(),
        ),
        out_specs=(P("gx", "gy", "gz"), P(None, "gx", "gy", "gz"), P("gx", "gy", "gz"), P()),
        check_vma=False,
    )
```

time: 121 us -> 31.2 us (0.26)
  blocking collectives: 44.5 us -> 0 us
  other arithmetic: 30.2 us -> 0 us
  Pallas kernels: 0 us -> 25.3 us
  starting transfers between devices: 19.9 us -> 0 us
  local copies, waits for them, and re-layouts: 20.8 us -> 5.02 us
  between operations: 3.16 us -> 0.64 us
  waiting for transfers between devices: 1.73 us -> 0 us
    psum x1 -> x0, blocking collectives: 44.5 us -> none  [shards(): lax.psum((jnp.sum(updated[0]), jnp.sum(updated[4])), ('gx', 'gy', 'gz'))]
    pallas_call x0 -> x1, Pallas kernels: none -> 25.3 us  [shards(): pl.pallas_call(functools.partial(kernel, sizes), out_shape=(jax.ShapeDtyp...]
    ppermute x9 -> x0, starting transfers between devices: 19.9 us -> none  [the longest x3 12 us: padded_2(): lax.ppermute(lax.slice_in_dim(block, block.shape[dim] - width, None, axis...]
    slice x16 -> x0, local copies, waits for them, and re-layouts: 12.5 us -> none  [the longest x5 5.54 us: padded_2(): lax.slice_in_dim(block, block.shape[dim] - width, None, axis=dim)]
    concatenate x9 -> x0, other arithmetic: 10.1 us -> none  [the longest x6 7.61 us: fix_ghosts(): jnp.concatenate([low_ghosts, lax.slice_in_dim(padded, 2, total_len - 2, a...]
    select_n x7 -> x0, other arithmetic: 8.88 us -> none  [the longest x3 4.44 us: fix_ghosts(): jnp.where(position == count_on - 1, jnp.concatenate([last_cell, last_cell...]
    mul x7 -> x0, other arithmetic: 6.04 us -> none  [the longest x3 2.57 us: flux_change(): face_rows * jnp.where(face_rows > 0, low_val + 0.5 * (1.0 - face_rows) *...]
    ppermute x2 -> x0, local copies, waits for them, and re-layouts: 4.69 us -> none  [the longest x1 2.36 us: padded_2(): lax.ppermute(lax.slice_in_dim(block, block.shape[dim] - width, None, axis...]
  transfers between devices with their start and end apart: 9 -> 0, of which waited for: 1 -> 0; matrix products, arithmetic and copies ran while one was open for 31% -> 0% of each run, Pallas kernels for 0% -> 0%
where the time goes in v1:
time: 31.2 us; the launch traced here: 31 us
  Pallas kernels  25.3 us (81%)
  local copies, waits for them, and re-layouts  5.02 us (16%)
  between operations  0.64 us (2%)
    pallas_call x1, Pallas kernels, shards(): pl.pallas_call(functools.partial(kernel, sizes), out_shape=(jax.ShapeDtyp...  25.3 us
    unnamed x8, local copies, waits for them, and re-layouts  5.02 us

profile of v1, /device:TPU:0, one launch (start us, length us, event | category | flops | bytes accessed | tf_op | source)
XLA Modules:
  0.0 31.0 jit_solution(9320486981347433327)
XLA Ops:
  0.6 25.3 %shard_map.84 = (f32[8,64,128]{2,1,0:T(8,128)}, f32[3,8,64,128]{3,2,1,0:T(8,128)}, f32[8,64,128]{2,1,0:T(8,128)}, f32[2]{0:T(128)}) custom-call(s32[6]{0:T(128)} %flags.1, f32[8,64,128]{2,1,0:T(8,128)} %den.1, f32[3,8,64,128]{3,2,1,0:T(8,128)} %mom.1, f32[8,64,128]{2,1,0:T(8,128)} %en.1, s32[3,8,64,128]{3,2,1,0:T(8,128)} %disp.1), custom_call_target="tpu_custom_call" | custom-call | tf_op jit(solution)/shard_map/pallas_call | solution.py:384
  26.0 1.7 %copy.13 = f32[8,64,128]{2,1,0:T(8,128)} copy(f32[8,64,128]{2,1,0:T(8,128)} %get-tuple-element.8) | data formatting | bytes 524288
  27.7 0.0 copy-start
  27.7 2.1 %copy.14 = f32[3,8,64,128]{3,2,1,0:T(8,128)} copy(f32[3,8,64,128]{3,2,1,0:T(8,128)} %get-tuple-element.9) | data formatting | bytes 1572864
  29.8 0.0 copy-done
  29.8 0.0 copy-start.1
  29.8 0.7 %copy.15 = f32[8,64,128]{2,1,0:T(8,128)} copy(f32[8,64,128]{2,1,0:T(8,128)S(1)} %copy-done) | data formatting | bytes 524288
  30.5 0.0 copy-done.1
  30.5 0.5 %copy.16 = f32[2]{0:T(128)} copy(f32[2]{0:T(128)S(1)} %copy-done.1) | data formatting | bytes 16
Async XLA Ops:
  27.7 2.1 %copy-start = (f32[8,64,128]{2,1,0:T(8,128)S(1)}, f32[8,64,128]{2,1,0:T(8,128)}, u32[]{:S(2)}) copy-start(f32[8,64,128]{2,1,0:T(8,128)} %get-tuple-element.10) | copy-start | bytes 786436
  29.8 0.7 %copy-start.1 = (f32[2]{0:T(128)S(1)}, f32[2]{0:T(128)}, u32[]{:S(2)}) copy-start(f32[2]{0:T(128)} %get-tuple-element.11) | copy-start | bytes 28

commit v2 on v1

--- a/solution.py
+++ b/solution.py
@@ -26,7 +26,7 @@
 
 
 def kernel(
-    sizes, flags, den, mom, en, disp, out_d, out_m, out_e, totals,
+    sizes, flags, den, mom, en, disp, out_d, out_m, out_e, sums,
     q, dx, dy, dz, xlo, xhi, xv, edge, zlo, zhi, cq, cs, sum_x, sum_y, sum_z,
     local_sem, send_sem, recv_sem, ssx, rsx, ssy, rsy, ssz, rsz,
 ):
@@ -36,9 +36,6 @@
     per = nz // 4
     parts = edge.shape[0]
     scale = 1.0 / 256.0
-    cells = float(nx * ny * nz)
-    for a in AXES:
-        cells = cells * sizes[a]
 
     locals_ = [
         pltpu.make_async_copy(den, q.at[0, :, SUB:top], local_sem.at[0]),
@@ -323,6 +320,27 @@
     sum_x[pos["gx"], 0] = a
     sum_x[pos["gx"], 1] = b
 
+    def core(r, _):
+        at = pl.ds(pl.multiple_of(r * SUB, SUB), SUB)
+        inner = pl.ds(pl.multiple_of(r * SUB + SUB, SUB), SUB)
+        vs = [dx[c, at].astype(jnp.float32) * scale for c in range(2, nx - 1)]
+        gs = [gain(v) for v in vs]
+        for f in range(5):
+            line_q = [q[f, c, inner] for c in range(nx)]
+            ds = [line_q[i + 1] - line_q[i] for i in range(nx - 1)]
+            ss = [minmod(ds[i + 1], ds[i]) for i in range(nx - 2)]
+            fl = [
+                flux(vs[i], gs[i], line_q[i + 1], line_q[i + 2], ss[i], ss[i + 1])
+                for i in range(nx - 3)
+            ]
+            for c in range(1, nx - 1):
+                change = fl[c - 2] if c >= 2 else 0.0
+                ref = outs[f](c)
+                ref[at] += change - fl[c - 1] if c < nx - 2 else change
+        return 0
+
+    lax.fori_loop(0, ny // SUB, core, 0)
+
     def x_low():
         xlo[...] = jnp.broadcast_to(q[:, 0:1, SUB:top], (5, 2, ny, nz))
 
@@ -335,39 +353,61 @@
     arrive("gx", x_up, x_down, x_low, x_high)
     x_lo_mult, x_hi_mult = low_mult(0) * scale, high_mult(0) * scale
 
-    def along_x(r, _):
-        at = pl.ds(pl.multiple_of(r * SUB, SUB), SUB)
-        inner = pl.ds(pl.multiple_of(r * SUB + SUB, SUB), SUB)
-        vs = [dx[c, at].astype(jnp.float32) * (x_lo_mult if c == 0 else scale) for c in range(nx)]
-        vs.append(xv[at].astype(jnp.float32) * x_hi_mult)
+    def x_rows(r):
+        return pl.ds(pl.multiple_of(r * SUB, SUB), SUB), pl.ds(
+            pl.multiple_of(r * SUB + SUB, SUB), SUB
+        )
+
+    def x_flux(v, g, cells4):
+        ds = [cells4[i + 1] - cells4[i] for i in range(3)]
+        return flux(
+            v, g, cells4[1], cells4[2], minmod(ds[1], ds[0]), minmod(ds[2], ds[1])
+        )
+
+    def rim(r, _):
+        at, inner = x_rows(r)
+        faces = (0, 1, nx - 1, nx)
+        vs = [
+            dx[0, at].astype(jnp.float32) * x_lo_mult,
+            dx[1, at].astype(jnp.float32) * scale,
+            dx[nx - 1, at].astype(jnp.float32) * scale,
+            xv[at].astype(jnp.float32) * x_hi_mult,
+        ]
         gs = [gain(v) for v in vs]
         for f in range(5):
-            line_q = (
-                [xlo[f, 0, at], xlo[f, 1, at]]
-                + [q[f, c, inner] for c in range(nx)]
-                + [xhi[f, 0, at], xhi[f, 1, at]]
-            )
-            ds = [line_q[i + 1] - line_q[i] for i in range(nx + 3)]
-            ss = [minmod(ds[i + 1], ds[i]) for i in range(nx + 2)]
-            fl = [
-                flux(vs[i], gs[i], line_q[i + 1], line_q[i + 2], ss[i], ss[i + 1])
-                for i in range(nx + 1)
-            ]
-            for c in range(nx):
+            a = [xlo[f, 0, at], xlo[f, 1, at]] + [q[f, c, inner] for c in range(3)]
+            b = [q[f, c, inner] for c in range(nx - 3, nx)] + [xhi[f, 0, at], xhi[f, 1, at]]
+            fl = [x_flux(vs[i], gs[i], (a, a, b, b)[i][i % 2 : i % 2 + 4]) for i in range(4)]
+            for c, change in (
+                (0, fl[0] - fl[1]), (1, fl[1]), (nx - 2, -fl[2]), (nx - 1, fl[2] - fl[3]),
+            ):
                 ref = outs[f](c)
-                ref[at] += fl[c] - fl[c + 1]
+                ref[at] += change
         return 0
 
-    lax.fori_loop(0, ny // SUB, along_x, 0)
+    lax.fori_loop(0, ny // SUB, rim, 0)
 
     a, b = collect("gx", sum_x, ssx, rsx)
-    totals[0] = jnp.sum(a) / cells
-    totals[1] = jnp.sum(b) / cells
+    sums[0] = a
+    sums[1] = b
     sent("gx", x_up, x_down)
     sent("gy", y_up, y_down)
     sent("gz", z_up, z_down)
     for c in line_x + line_y + line_z:
         c.wait_send()
+
+
+def put(cells, den, mom, en, sums, out_d, out_m, out_e, totals, sem):
+    moves = [
+        pltpu.make_async_copy(src, dst, sem.at[i])
+        for i, (src, dst) in enumerate(((mom, out_m), (den, out_d), (en, out_e)))
+    ]
+    for c in moves:
+        c.start()
+    totals[0] = jnp.sum(sums[0]) / cells
+    totals[1] = jnp.sum(sums[1]) / cells
+    for c in moves:
+        c.wait()
 
 
 def shards(density, momentum, energy, displacement, flags):
@@ -379,18 +419,18 @@
     f32, i32 = jnp.float32, jnp.int32
     dma = pltpu.SemaphoreType.DMA
     any_ = pl.BlockSpec(memory_space=pl.ANY)
+    hbm = pl.BlockSpec(memory_space=pltpu.HBM)
     vmem = pl.BlockSpec(memory_space=pltpu.VMEM)
     smem = pl.BlockSpec(memory_space=pltpu.SMEM)
-    return pl.pallas_call(
+    cells = float(nx * ny * nz)
+    for a in AXES:
+        cells = cells * sizes[a]
+    outputs = tuple(jax.ShapeDtypeStruct(v.shape, f32) for v in (density, momentum, energy))
+    results = pl.pallas_call(
         functools.partial(kernel, sizes),
-        out_shape=(
-            jax.ShapeDtypeStruct(density.shape, f32),
-            jax.ShapeDtypeStruct(momentum.shape, f32),
-            jax.ShapeDtypeStruct(energy.shape, f32),
-            jax.ShapeDtypeStruct((2,), f32),
-        ),
-        in_specs=[smem, any_, any_, any_, any_],
-        out_specs=(vmem, vmem, vmem, smem),
+        out_shape=outputs + (jax.ShapeDtypeStruct((2, SUB, nz), f32),),
+        in_specs=[smem, hbm, hbm, hbm, hbm],
+        out_specs=(vmem, vmem, vmem, vmem),
         scratch_shapes=[
             pltpu.VMEM((5, nx, tall, nz), f32),
             pltpu.VMEM((nx, ny, nz), i32),
@@ -404,8 +444,18 @@
         + [pltpu.VMEM((sizes[a], 2, SUB, nz), f32) for a in AXES]
         + [dma((6,)), dma((16,)), dma((16,))]
         + [dma((sizes[a],)) for a in AXES for _ in range(2)],
-        compiler_params=pltpu.CompilerParams(collective_id=0, has_side_effects=True),
-    )(flags, density, momentum, energy, displacement)
+        compiler_params=pltpu.CompilerParams(
+            collective_id=0, has_side_effects=True, vmem_limit_bytes=12 << 20
+        ),
+    )(flags, *(pltpu.with_memory_space_constraint(v, pltpu.HBM) for v in (density, momentum, energy, displacement)))
+    return pl.pallas_call(
+        functools.partial(put, cells),
+        out_shape=outputs + (jax.ShapeDtypeStruct((2,), f32),),
+        in_specs=[any_, any_, any_, vmem],
+        out_specs=(hbm, hbm, hbm, smem),
+        scratch_shapes=[dma((3,))],
+        compiler_params=pltpu.CompilerParams(vmem_limit_bytes=2 << 20),
+    )(*results)
 
 
 def solution(mesh):

time: 31.2 us -> 26.7 us (0.86)
  local copies, waits for them, and re-layouts: 5.02 us -> 0.65 us
    unnamed x8 -> x2, local copies, waits for them, and re-layouts: 5.02 us -> 0.65 us
    pallas_call x1 -> x2, Pallas kernels: 25.3 us -> 25.3 us  [the longest x1 23.7 us: shards(): pl.pallas_call(functools.partial(kernel, sizes), out_shape=outputs + (jax...]
where the time goes in v2:
time: 26.7 us; the launch traced here: 26.6 us
  Pallas kernels  25.3 us (95%)
  local copies, waits for them, and re-layouts  0.65 us (2%)
  between operations  0.65 us (2%)
    pallas_call x1, Pallas kernels, shards(): pl.pallas_call(functools.partial(kernel, sizes), out_shape=outputs + (jax...  23.7 us
    pallas_call x1, Pallas kernels, shards(): pl.pallas_call(functools.partial(put, cells), out_shape=outputs + (jax.Sh...  1.59 us
    unnamed x2, local copies, waits for them, and re-layouts  0.65 us

profile of v2, /device:TPU:0, one launch (start us, length us, event | category | flops | bytes accessed | tf_op | source)
XLA Modules:
  0.0 26.6 jit_solution(10518511624833219418)
XLA Ops:
  0.6 0.0 copy-start
  0.6 0.6 %copy-done = s32[6]{0:T(128)S(1)} copy-done((s32[6]{0:T(128)S(1)}, s32[6]{0:T(128)}, u32[]{:S(2)}) %copy-start) | copy-done | bytes 48
  1.3 23.7 %shard_map.84 = (f32[8,64,128]{2,1,0:T(8,128)S(1)}, f32[3,8,64,128]{3,2,1,0:T(8,128)S(1)}, f32[8,64,128]{2,1,0:T(8,128)S(1)}, f32[2,8,128]{2,1,0:T(8,128)S(1)}) custom-call(s32[6]{0:T(128)S(1)} %copy-done, f32[8,64,128]{2,1,0:T(8,128)} %den.1, f32[3,8,64,128]{3,2,1,0:T(8,128)} %mom.1, f32[8,64,128]{2,1,0:T(8,128)} %en.1, s32[3,8,64,128]{3,2,1,0:T(8,128)} %disp.1), custom_call_target="tpu_custom_call" | custom-call | tf_op jit(solution)/shard_map/pallas_call | solution.py:429
  25.0 1.6 %shard_map.85 = (f32[8,64,128]{2,1,0:T(8,128)}, f32[3,8,64,128]{3,2,1,0:T(8,128)}, f32[8,64,128]{2,1,0:T(8,128)}, f32[2]{0:T(128)}) custom-call(f32[8,64,128]{2,1,0:T(8,128)S(1)} %get-tuple-element.8.den, f32[3,8,64,128]{3,2,1,0:T(8,128)S(1)} %get-tuple-element.9.mom, f32[8,64,128]{2,1,0:T(8,128)S(1)} %get-tuple-element.10.en, ...), custom_call_target="tpu_custom_call" | custom-call | tf_op jit(solution)/shard_map/pallas_call | solution.py:451
Async XLA Ops:
  0.6 0.7 %copy-start = (s32[6]{0:T(128)S(1)}, s32[6]{0:T(128)}, u32[]{:S(2)}) copy-start(s32[6]{0:T(128)} %flags.1) | copy-start | bytes 76

commit v3 on v2

--- a/solution.py
+++ b/solution.py
@@ -26,8 +26,8 @@
 
 
 def kernel(
-    sizes, flags, den, mom, en, disp, out_d, out_m, out_e, sums,
-    q, dx, dy, dz, xlo, xhi, xv, edge, zlo, zhi, cq, cs, sum_x, sum_y, sum_z,
+    sizes, flags_in, den, mom, en, disp, out_d, out_m, out_e, sums,
+    flags, q, dx, dy, dz, xh, hop, xv, edge, zlo, zhi, cq, cs, sum_x, sum_y, sum_z,
     local_sem, send_sem, recv_sem, ssx, rsx, ssy, rsy, ssz, rsz,
 ):
     nx, ny, nz = den.shape
@@ -36,6 +36,7 @@
     per = nz // 4
     parts = edge.shape[0]
     scale = 1.0 / 256.0
+    xlo, xhi = xh.at[0], xh.at[1]
 
     locals_ = [
         pltpu.make_async_copy(den, q.at[0, :, SUB:top], local_sem.at[0]),
@@ -44,6 +45,7 @@
         pltpu.make_async_copy(disp.at[2], dz, local_sem.at[3]),
         pltpu.make_async_copy(disp.at[1], dy.at[:, SUB:top], local_sem.at[4]),
         pltpu.make_async_copy(disp.at[0], dx, local_sem.at[5]),
+        pltpu.make_async_copy(flags_in, flags, local_sem.at[6]),
     ]
     for c in locals_:
         c.start()
@@ -66,17 +68,72 @@
         )
 
     last = {a: sizes[a] - 1 for a in AXES}
+    me = pos["gx"]
+    par = lax.rem(me, 2)
+    odd = par == 1
+    end = last["gx"]
+    leg_out = (odd & (me + 2 <= end)) | ((par == 0) & (me >= 2))
+    relays = (odd & (me >= 3)) | ((par == 0) & (me + 2 <= end))
+    leg_in = (me + 1 <= end) & (odd | (me >= 2))
+    begin = par * (nx - 2)
+    other = 1 - par
+
+    def remote(k, src, dst, target):
+        return pltpu.make_async_remote_copy(
+            src_ref=src, dst_ref=dst, send_sem=send_sem.at[k], recv_sem=recv_sem.at[k],
+            device_id={"gx": target}, device_id_type=pl.DeviceIdType.MESH,
+        )
+
+    over = me + 4 * par - 2
+    legs = [
+        remote(16, mom.at[0, pl.ds(begin, 2)], hop.at[0:2], over),
+        remote(17, mom.at[1, pl.ds(begin, 2)], hop.at[2:4], over),
+        remote(18, en.at[begin], hop.at[4], over),
+    ]
+    beside = me + 1 - 2 * par
+    onward = [
+        remote(19, hop.at[0:2], xh.at[other, 1], beside),
+        remote(20, hop.at[2:4], xh.at[other, 2], beside),
+        remote(21, hop.at[4], xh.at[other, 4, 0], beside),
+    ]
+    landed = [
+        remote(19, hop.at[0:2], xh.at[par, 1], beside),
+        remote(20, hop.at[2:4], xh.at[par, 2], beside),
+        remote(21, hop.at[4], xh.at[par, 4, 0], beside),
+    ]
     x_up = [
         copy(0, den.at[nx - 2 : nx], xlo.at[0], "gx", 1),
-        copy(1, mom.at[:, nx - 2 : nx], xlo.at[1:4], "gx", 1),
-        copy(2, en.at[nx - 2 : nx], xlo.at[4], "gx", 1),
+        copy(1, mom.at[2, nx - 2 : nx], xlo.at[3], "gx", 1),
+        copy(2, en.at[nx - 1], xlo.at[4, 1], "gx", 1),
+    ]
+    x_up_half = [
+        copy(22, mom.at[0:2, nx - 2 : nx], xlo.at[1:3], "gx", 1),
+        copy(23, en.at[nx - 2], xlo.at[4, 0], "gx", 1),
     ]
     x_down = [
+        copy(6, disp.at[0, 0], xv, "gx", -1),
         copy(3, den.at[0:2], xhi.at[0], "gx", -1),
-        copy(4, mom.at[:, 0:2], xhi.at[1:4], "gx", -1),
-        copy(5, en.at[0:2], xhi.at[4], "gx", -1),
-        copy(6, disp.at[0, 0], xv, "gx", -1),
-    ]
+        copy(4, mom.at[2, 0:2], xhi.at[3], "gx", -1),
+        copy(5, en.at[1], xhi.at[4, 1], "gx", -1),
+    ]
+    x_down_half = [
+        copy(24, mom.at[0:2, 0:2], xhi.at[1:3], "gx", -1),
+        copy(25, en.at[0], xhi.at[4, 0], "gx", -1),
+    ]
+    up_half = (me < end) & ~(leg_out & odd)
+    down_half = (me > 0) & ~(leg_out & (par == 0))
+    low_half = (me > 0) & ~(leg_in & (par == 0))
+    high_half = (me < end) & ~(leg_in & odd)
+
+    def each(cond, copies, act):
+        @pl.when(cond)
+        def _():
+            for c in copies:
+                act(c)
+
+    def go(c):
+        c.start()
+
     hi_rows = slice(top, top + SUB)
     y_up = [
         copy(7, den.at[:, ny - SUB : ny], q.at[0, :, 0:SUB], "gy", 1),
@@ -133,8 +190,16 @@
             for c in downs:
                 c.wait_send()
 
-    start("gx", x_up, x_down)
+    each(leg_out, legs, go)
+    each(odd & (me < end), x_up, go)
+    each(me > 0, x_down, go)
+    each((par == 0) & (me < end), x_up, go)
+    each(up_half, x_up_half, go)
+    each(down_half, x_down_half, go)
     start("gy", y_up, y_down)
+
+    for c in locals_:
+        c.wait()
 
     flag = [flags[i].astype(jnp.float32) for i in range(6)]
 
@@ -149,9 +214,6 @@
 
     def outer_high(a):
         return jnp.where(pos[AXES[a]] == last[AXES[a]], flag[2 * a + 1], 0.0)
-
-    for c in locals_:
-        c.wait()
 
     lane = lax.broadcasted_iota(jnp.int32, (ny, nz), 1)
     row = lax.broadcasted_iota(jnp.int32, (ny, nz), 0)
@@ -279,6 +341,12 @@
         return 0
 
     lax.fori_loop(0, nx, along_z, 0)
+
+    @pl.when(relays)
+    def _():
+        for a, b in zip(legs, onward):
+            a.wait_recv()
+            b.start()
 
     a, b = collect("gz", sum_z, ssz, rsz)
     sum_y[pos["gy"], 0] = a
@@ -350,6 +418,9 @@
 
     for c in line_x:
         c.start()
+    each(low_half, x_up_half, lambda c: c.wait_recv())
+    each(high_half, x_down_half, lambda c: c.wait_recv())
+    each(leg_in, landed, lambda c: c.wait_recv())
     arrive("gx", x_up, x_down, x_low, x_high)
     x_lo_mult, x_hi_mult = low_mult(0) * scale, high_mult(0) * scale
 
@@ -391,6 +462,10 @@
     sums[0] = a
     sums[1] = b
     sent("gx", x_up, x_down)
+    each(leg_out, legs, lambda c: c.wait_send())
+    each(relays, onward, lambda c: c.wait_send())
+    each(up_half, x_up_half, lambda c: c.wait_send())
+    each(down_half, x_down_half, lambda c: c.wait_send())
     sent("gy", y_up, y_down)
     sent("gz", z_up, z_down)
     for c in line_x + line_y + line_z:
@@ -429,25 +504,31 @@
     results = pl.pallas_call(
         functools.partial(kernel, sizes),
         out_shape=outputs + (jax.ShapeDtypeStruct((2, SUB, nz), f32),),
-        in_specs=[smem, hbm, hbm, hbm, hbm],
+        in_specs=[hbm] * 5,
         out_specs=(vmem, vmem, vmem, vmem),
         scratch_shapes=[
+            pltpu.SMEM((6,), i32),
             pltpu.VMEM((5, nx, tall, nz), f32),
             pltpu.VMEM((nx, ny, nz), i32),
             pltpu.VMEM((nx, tall, nz), i32),
             pltpu.VMEM((nx, ny, nz), i32),
-            pltpu.VMEM((5, 2, ny, nz), f32),
-            pltpu.VMEM((5, 2, ny, nz), f32),
+            pltpu.VMEM((2, 5, 2, ny, nz), f32),
+            pltpu.VMEM((5, ny, nz), f32),
             pltpu.VMEM((ny, nz), i32),
         ]
         + [pltpu.VMEM((parts, ny, nz), f32) for _ in range(5)]
         + [pltpu.VMEM((sizes[a], 2, SUB, nz), f32) for a in AXES]
-        + [dma((6,)), dma((16,)), dma((16,))]
+        + [dma((7,)), dma((26,)), dma((26,))]
         + [dma((sizes[a],)) for a in AXES for _ in range(2)],
         compiler_params=pltpu.CompilerParams(
             collective_id=0, has_side_effects=True, vmem_limit_bytes=12 << 20
         ),
-    )(flags, *(pltpu.with_memory_space_constraint(v, pltpu.HBM) for v in (density, momentum, energy, displacement)))
+    )(
+        *(
+            pltpu.with_memory_space_constraint(v, pltpu.HBM)
+            for v in (flags, density, momentum, energy, displacement)
+        )
+    )
     return pl.pallas_call(
         functools.partial(put, cells),
         out_shape=outputs + (jax.ShapeDtypeStruct((2,), f32),),

time: 26.7 us -> 22.8 us (0.85)
  Pallas kernels: 25.3 us -> 22.1 us
  local copies, waits for them, and re-layouts: 0.65 us -> 0 us
    pallas_call x1, Pallas kernels: 23.7 us -> 20.5 us  [shards(): pl.pallas_call(functools.partial(kernel, sizes), out_shape=outputs + (jax...]
    unnamed x2 -> x0, local copies, waits for them, and re-layouts: 0.65 us -> none
where the time goes in v3:
time: 22.8 us; the launch traced here: 22.7 us
  Pallas kernels  22.1 us (97%)
  between operations  0.64 us (3%)
    pallas_call x1, Pallas kernels, shards(): pl.pallas_call(functools.partial(kernel, sizes), out_shape=outputs + (jax...  20.5 us
    pallas_call x1, Pallas kernels, shards(): pl.pallas_call(functools.partial(put, cells), out_shape=outputs + (jax.Sh...  1.59 us

profile of v3, /device:TPU:0, one launch (start us, length us, event | category | flops | bytes accessed | tf_op | source)
XLA Modules:
  0.0 22.7 jit_solution(17705543608912344243)
XLA Ops:
  0.6 20.5 %shard_map.84 = (f32[8,64,128]{2,1,0:T(8,128)S(1)}, f32[3,8,64,128]{3,2,1,0:T(8,128)S(1)}, f32[8,64,128]{2,1,0:T(8,128)S(1)}, f32[2,8,128]{2,1,0:T(8,128)S(1)}) custom-call(s32[6]{0:T(128)} %flags_in.1, f32[8,64,128]{2,1,0:T(8,128)} %den.1, f32[3,8,64,128]{3,2,1,0:T(8,128)} %mom.1, f32[8,64,128]{2,1,0:T(8,128)} %en.1, s32[3,8,64,128]{3,2,1,0:T(8,128)} %disp.1), custom_call_target="tpu_custom_call" | custom-call | tf_op jit(solution)/shard_map/pallas_call | solution.py:504
  21.1 1.6 %shard_map.85 = (f32[8,64,128]{2,1,0:T(8,128)}, f32[3,8,64,128]{3,2,1,0:T(8,128)}, f32[8,64,128]{2,1,0:T(8,128)}, f32[2]{0:T(128)}) custom-call(f32[8,64,128]{2,1,0:T(8,128)S(1)} %get-tuple-element.8.den, f32[3,8,64,128]{3,2,1,0:T(8,128)S(1)} %get-tuple-element.9.mom, f32[8,64,128]{2,1,0:T(8,128)S(1)} %get-tuple-element.10.en, ...), custom_call_target="tpu_custom_call" | custom-call | tf_op jit(solution)/shard_map/pallas_call | solution.py:532

commit v4 on v3

--- a/solution.py
+++ b/solution.py
@@ -38,6 +38,16 @@
     scale = 1.0 / 256.0
     xlo, xhi = xh.at[0], xh.at[1]
 
+    barrier = pltpu.get_barrier_semaphore()
+    greeted = 0
+    for a in ("gy", "gx", "gz"):
+        for o in range(1, sizes[a]):
+            peer = lax.rem(pos[a] + o, sizes[a])
+            pl.semaphore_signal(
+                barrier, inc=1, device_id={a: peer}, device_id_type=pl.DeviceIdType.MESH
+            )
+            greeted += 1
+
     locals_ = [
         pltpu.make_async_copy(den, q.at[0, :, SUB:top], local_sem.at[0]),
         pltpu.make_async_copy(mom, q.at[1:4, :, SUB:top], local_sem.at[1]),
@@ -50,15 +60,6 @@
     for c in locals_:
         c.start()
 
-    barrier = pltpu.get_barrier_semaphore()
-    greeted = 0
-    for a in AXES:
-        for o in range(1, sizes[a]):
-            peer = lax.rem(pos[a] + o, sizes[a])
-            pl.semaphore_signal(
-                barrier, inc=1, device_id={a: peer}, device_id_type=pl.DeviceIdType.MESH
-            )
-            greeted += 1
     pl.semaphore_wait(barrier, greeted)
 
     def copy(k, src, dst, axis, step):
@@ -418,9 +419,6 @@
 
     for c in line_x:
         c.start()
-    each(low_half, x_up_half, lambda c: c.wait_recv())
-    each(high_half, x_down_half, lambda c: c.wait_recv())
-    each(leg_in, landed, lambda c: c.wait_recv())
     arrive("gx", x_up, x_down, x_low, x_high)
     x_lo_mult, x_hi_mult = low_mult(0) * scale, high_mult(0) * scale
 
@@ -435,7 +433,7 @@
             v, g, cells4[1], cells4[2], minmod(ds[1], ds[0]), minmod(ds[2], ds[1])
         )
 
-    def rim(r, _):
+    def rim(fields, r, _):
         at, inner = x_rows(r)
         faces = (0, 1, nx - 1, nx)
         vs = [
@@ -445,7 +443,7 @@
             xv[at].astype(jnp.float32) * x_hi_mult,
         ]
         gs = [gain(v) for v in vs]
-        for f in range(5):
+        for f in fields:
             a = [xlo[f, 0, at], xlo[f, 1, at]] + [q[f, c, inner] for c in range(3)]
             b = [q[f, c, inner] for c in range(nx - 3, nx)] + [xhi[f, 0, at], xhi[f, 1, at]]
             fl = [x_flux(vs[i], gs[i], (a, a, b, b)[i][i % 2 : i % 2 + 4]) for i in range(4)]
@@ -456,7 +454,11 @@
                 ref[at] += change
         return 0
 
-    lax.fori_loop(0, ny // SUB, rim, 0)
+    lax.fori_loop(0, ny // SUB, functools.partial(rim, (0, 3)), 0)
+    each(low_half, x_up_half, lambda c: c.wait_recv())
+    each(high_half, x_down_half, lambda c: c.wait_recv())
+    each(leg_in, landed, lambda c: c.wait_recv())
+    lax.fori_loop(0, ny // SUB, functools.partial(rim, (1, 2, 4)), 0)
 
     a, b = collect("gx", sum_x, ssx, rsx)
     sums[0] = a
@@ -473,9 +475,15 @@
 
 
 def put(cells, den, mom, en, sums, out_d, out_m, out_e, totals, sem):
+    pairs = [(den, out_d), (en, out_e)] + [(mom.at[c], out_m.at[c]) for c in range(3)]
+    half = den.shape[0] // 2
+    pairs = [
+        (src.at[at], dst.at[at])
+        for src, dst in pairs
+        for at in (slice(0, half), slice(half, 2 * half))
+    ]
     moves = [
-        pltpu.make_async_copy(src, dst, sem.at[i])
-        for i, (src, dst) in enumerate(((mom, out_m), (den, out_d), (en, out_e)))
+        pltpu.make_async_copy(src, dst, sem.at[i]) for i, (src, dst) in enumerate(pairs)
     ]
     for c in moves:
         c.start()
@@ -534,7 +542,7 @@
         out_shape=outputs + (jax.ShapeDtypeStruct((2,), f32),),
         in_specs=[any_, any_, any_, vmem],
         out_specs=(hbm, hbm, hbm, smem),
-        scratch_shapes=[dma((3,))],
+        scratch_shapes=[dma((10,))],
         compiler_params=pltpu.CompilerParams(vmem_limit_bytes=2 << 20),
     )(*results)
 

time: 22.8 us -> 22.9 us (level)
  no operation moved by 1% of the time
where the time goes in v4:
time: 22.9 us; the launch traced here: 22.7 us
  Pallas kernels  22.1 us (97%)
  between operations  0.64 us (3%)
    pallas_call x1, Pallas kernels, shards(): pl.pallas_call(functools.partial(kernel, sizes), out_shape=outputs + (jax...  20.4 us
    pallas_call x1, Pallas kernels, shards(): pl.pallas_call(functools.partial(put, cells), out_shape=outputs + (jax.Sh...  1.65 us

profile of v4, /device:TPU:0, one launch (start us, length us, event | category | flops | bytes accessed | tf_op | source)
XLA Modules:
  0.0 22.7 jit_solution(8440187751836099975)
XLA Ops:
  0.6 20.4 %shard_map.84 = (f32[8,64,128]{2,1,0:T(8,128)S(1)}, f32[3,8,64,128]{3,2,1,0:T(8,128)S(1)}, f32[8,64,128]{2,1,0:T(8,128)S(1)}, f32[2,8,128]{2,1,0:T(8,128)S(1)}) custom-call(s32[6]{0:T(128)} %flags_in.1, f32[8,64,128]{2,1,0:T(8,128)} %den.1, f32[3,8,64,128]{3,2,1,0:T(8,128)} %mom.1, f32[8,64,128]{2,1,0:T(8,128)} %en.1, s32[3,8,64,128]{3,2,1,0:T(8,128)} %disp.1), custom_call_target="tpu_custom_call" | custom-call | tf_op jit(solution)/shard_map/pallas_call | solution.py:512
  21.1 1.6 %shard_map.85 = (f32[8,64,128]{2,1,0:T(8,128)}, f32[3,8,64,128]{3,2,1,0:T(8,128)}, f32[8,64,128]{2,1,0:T(8,128)}, f32[2]{0:T(128)}) custom-call(f32[8,64,128]{2,1,0:T(8,128)S(1)} %get-tuple-element.8.den, f32[3,8,64,128]{3,2,1,0:T(8,128)S(1)} %get-tuple-element.9.mom, f32[8,64,128]{2,1,0:T(8,128)S(1)} %get-tuple-element.10.en, ...), custom_call_target="tpu_custom_call" | custom-call | tf_op jit(solution)/shard_map/pallas_call | solution.py:540

commit v5 on v4

--- a/solution.py
+++ b/solution.py
@@ -39,14 +39,33 @@
     xlo, xhi = xh.at[0], xh.at[1]
 
     barrier = pltpu.get_barrier_semaphore()
+    doubling = sizes["gy"] & (sizes["gy"] - 1) == 0
+    strides = [1 << i for i in range(sizes["gy"].bit_length() - 1)] if doubling else []
+
+    def across(stride):
+        return pos["gy"] + stride - 2 * stride * lax.rem(pos["gy"] // stride, 2)
+
+    def greet(axis, peer):
+        pl.semaphore_signal(
+            barrier, inc=1, device_id={axis: peer}, device_id_type=pl.DeviceIdType.MESH
+        )
+
     greeted = 0
-    for a in ("gy", "gx", "gz"):
-        for o in range(1, sizes[a]):
-            peer = lax.rem(pos[a] + o, sizes[a])
-            pl.semaphore_signal(
-                barrier, inc=1, device_id={a: peer}, device_id_type=pl.DeviceIdType.MESH
-            )
-            greeted += 1
+    for a in ("gx", "gy", "gz"):
+        if a == "gy" and doubling:
+            for stride in strides:
+                greet(a, across(stride))
+                greeted += 1
+            for step in (1, -1):
+                @pl.when((pos[a] + step >= 0) & (pos[a] + step < sizes[a]))
+                def _():
+                    greet(a, pos[a] + step)
+
+            greeted += jnp.where(pos[a] > 0, 1, 0) + jnp.where(pos[a] < sizes[a] - 1, 1, 0)
+        else:
+            for o in range(1, sizes[a]):
+                greet(a, lax.rem(pos[a] + o, sizes[a]))
+                greeted += 1
 
     locals_ = [
         pltpu.make_async_copy(den, q.at[0, :, SUB:top], local_sem.at[0]),
@@ -288,7 +307,26 @@
         return a, b
 
     line_z = line("gz", sum_z, ssz, rsz)
-    line_y = line("gy", sum_y, ssy, rsy)
+    hops = [
+        pltpu.make_async_remote_copy(
+            src_ref=sum_y.at[2 * i], dst_ref=sum_y.at[2 * i + 1], send_sem=ssy.at[i],
+            recv_sem=rsy.at[i], device_id={"gy": across(stride)},
+            device_id_type=pl.DeviceIdType.MESH,
+        )
+        for i, stride in enumerate(strides)
+    ]
+    line_y = hops if doubling else line("gy", sum_y, ssy, rsy)
+
+    def step_y(i):
+        hops[i].wait_recv()
+        a = sum_y[2 * i, 0] + sum_y[2 * i + 1, 0]
+        b = sum_y[2 * i, 1] + sum_y[2 * i + 1, 1]
+        if i + 1 < len(hops):
+            sum_y[2 * i + 2, 0] = a
+            sum_y[2 * i + 2, 1] = b
+            hops[i + 1].start()
+        return a, b
+
     line_x = line("gx", sum_x, ssx, rsx)
     for c in line_z:
         c.start()
@@ -350,8 +388,9 @@
             b.start()
 
     a, b = collect("gz", sum_z, ssz, rsz)
-    sum_y[pos["gy"], 0] = a
-    sum_y[pos["gy"], 1] = b
+    own = 0 if doubling else pos["gy"]
+    sum_y[own, 0] = a
+    sum_y[own, 1] = b
 
     def y_low():
         q[:, :, 0:SUB] = jnp.broadcast_to(q[:, :, SUB : SUB + 1], (5, nx, SUB, nz))
@@ -361,7 +400,7 @@
         dy[:, hi_rows] = jnp.broadcast_to(dy[:, top - 1 : top], (nx, SUB, nz))
 
     arrive("gy", y_up, y_down, y_low, y_high)
-    for c in line_y:
+    for c in line_y[:1] if doubling else line_y:
         c.start()
     tall = ny + 2 * SUB
     rows = lax.broadcasted_iota(jnp.int32, (tall, nz), 0)
@@ -385,9 +424,8 @@
 
     lax.fori_loop(0, nx, along_y, 0)
 
-    a, b = collect("gy", sum_y, ssy, rsy)
-    sum_x[pos["gx"], 0] = a
-    sum_x[pos["gx"], 1] = b
+    if hops:
+        a, b = step_y(0)
 
     def core(r, _):
         at = pl.ds(pl.multiple_of(r * SUB, SUB), SUB)
@@ -417,6 +455,12 @@
         xhi[...] = jnp.broadcast_to(q[:, nx - 1 : nx, SUB:top], (5, 2, ny, nz))
         xv[...] = dx[nx - 1]
 
+    if not doubling:
+        a, b = collect("gy", sum_y, ssy, rsy)
+    for i in range(1, len(hops)):
+        a, b = step_y(i)
+    sum_x[pos["gx"], 0] = a
+    sum_x[pos["gx"], 1] = b
     for c in line_x:
         c.start()
     arrive("gx", x_up, x_down, x_low, x_high)

time: 22.9 us -> 23.8 us (1.039)
  Pallas kernels: 22.1 us -> 23 us
    pallas_call x1, Pallas kernels: 20.4 us -> 21.4 us  [shards(): pl.pallas_call(functools.partial(kernel, sizes), out_shape=outputs + (jax...]
where the time goes in v5:
time: 23.8 us; the launch traced here: 23.7 us
  Pallas kernels  23 us (97%)
  between operations  0.64 us (3%)
    pallas_call x1, Pallas kernels, shards(): pl.pallas_call(functools.partial(kernel, sizes), out_shape=outputs + (jax...  21.4 us
    pallas_call x1, Pallas kernels, shards(): pl.pallas_call(functools.partial(put, cells), out_shape=outputs + (jax.Sh...  1.65 us

profile of v5, /device:TPU:0, one launch (start us, length us, event | category | flops | bytes accessed | tf_op | source)
XLA Modules:
  0.0 23.7 jit_solution(14912511913049557231)
XLA Ops:
  0.6 21.4 %shard_map.84 = (f32[8,64,128]{2,1,0:T(8,128)S(1)}, f32[3,8,64,128]{3,2,1,0:T(8,128)S(1)}, f32[8,64,128]{2,1,0:T(8,128)S(1)}, f32[2,8,128]{2,1,0:T(8,128)S(1)}) custom-call(s32[6]{0:T(128)} %flags_in.1, f32[8,64,128]{2,1,0:T(8,128)} %den.1, f32[3,8,64,128]{3,2,1,0:T(8,128)} %mom.1, f32[8,64,128]{2,1,0:T(8,128)} %en.1, s32[3,8,64,128]{3,2,1,0:T(8,128)} %disp.1), custom_call_target="tpu_custom_call" | custom-call | tf_op jit(solution)/shard_map/pallas_call | solution.py:556
  22.0 1.6 %shard_map.85 = (f32[8,64,128]{2,1,0:T(8,128)}, f32[3,8,64,128]{3,2,1,0:T(8,128)}, f32[8,64,128]{2,1,0:T(8,128)}, f32[2]{0:T(128)}) custom-call(f32[8,64,128]{2,1,0:T(8,128)S(1)} %get-tuple-element.8.den, f32[3,8,64,128]{3,2,1,0:T(8,128)S(1)} %get-tuple-element.9.mom, f32[8,64,128]{2,1,0:T(8,128)S(1)} %get-tuple-element.10.en, ...), custom_call_target="tpu_custom_call" | custom-call | tf_op jit(solution)/shard_map/pallas_call | solution.py:584

commit v6 on v4

--- a/solution.py
+++ b/solution.py
@@ -455,10 +455,11 @@
         return 0
 
     lax.fori_loop(0, ny // SUB, functools.partial(rim, (0, 3)), 0)
-    each(low_half, x_up_half, lambda c: c.wait_recv())
-    each(high_half, x_down_half, lambda c: c.wait_recv())
-    each(leg_in, landed, lambda c: c.wait_recv())
-    lax.fori_loop(0, ny // SUB, functools.partial(rim, (1, 2, 4)), 0)
+    for part, whole, fields in ((0, (0,), (1,)), (1, (), (2,)), (2, (1,), (4,))):
+        each(low_half, [x_up_half[k] for k in whole], lambda c: c.wait_recv())
+        each(high_half, [x_down_half[k] for k in whole], lambda c: c.wait_recv())
+        each(leg_in, landed[part : part + 1], lambda c: c.wait_recv())
+        lax.fori_loop(0, ny // SUB, functools.partial(rim, fields), 0)
 
     a, b = collect("gx", sum_x, ssx, rsx)
     sums[0] = a
@@ -475,13 +476,7 @@
 
 
 def put(cells, den, mom, en, sums, out_d, out_m, out_e, totals, sem):
-    pairs = [(den, out_d), (en, out_e)] + [(mom.at[c], out_m.at[c]) for c in range(3)]
-    half = den.shape[0] // 2
-    pairs = [
-        (src.at[at], dst.at[at])
-        for src, dst in pairs
-        for at in (slice(0, half), slice(half, 2 * half))
-    ]
+    pairs = ((mom, out_m), (den, out_d), (en, out_e))
     moves = [
         pltpu.make_async_copy(src, dst, sem.at[i]) for i, (src, dst) in enumerate(pairs)
     ]
@@ -542,7 +537,7 @@
         out_shape=outputs + (jax.ShapeDtypeStruct((2,), f32),),
         in_specs=[any_, any_, any_, vmem],
         out_specs=(hbm, hbm, hbm, smem),
-        scratch_shapes=[dma((10,))],
+        scratch_shapes=[dma((3,))],
         compiler_params=pltpu.CompilerParams(vmem_limit_bytes=2 << 20),
     )(*results)
 

time: 22.9 us -> 22.8 us (level)
  no operation moved by 1% of the time
where the time goes in v6:
time: 22.8 us; the launch traced here: 22.7 us
  Pallas kernels  22 us (96%)
  between operations  0.64 us (3%)
    pallas_call x1, Pallas kernels, shards(): pl.pallas_call(functools.partial(kernel, sizes), out_shape=outputs + (jax...  20.4 us
    pallas_call x1, Pallas kernels, shards(): pl.pallas_call(functools.partial(put, cells), out_shape=outputs + (jax.Sh...  1.59 us

profile of v6, /device:TPU:0, one launch (start us, length us, event | category | flops | bytes accessed | tf_op | source)
XLA Modules:
  0.0 22.7 jit_solution(1112613870383898788)
XLA Ops:
  0.6 20.4 %shard_map.84 = (f32[8,64,128]{2,1,0:T(8,128)S(1)}, f32[3,8,64,128]{3,2,1,0:T(8,128)S(1)}, f32[8,64,128]{2,1,0:T(8,128)S(1)}, f32[2,8,128]{2,1,0:T(8,128)S(1)}) custom-call(s32[6]{0:T(128)} %flags_in.1, f32[8,64,128]{2,1,0:T(8,128)} %den.1, f32[3,8,64,128]{3,2,1,0:T(8,128)} %mom.1, f32[8,64,128]{2,1,0:T(8,128)} %en.1, s32[3,8,64,128]{3,2,1,0:T(8,128)} %disp.1), custom_call_target="tpu_custom_call" | custom-call | tf_op jit(solution)/shard_map/pallas_call | solution.py:507
  21.1 1.6 %shard_map.85 = (f32[8,64,128]{2,1,0:T(8,128)}, f32[3,8,64,128]{3,2,1,0:T(8,128)}, f32[8,64,128]{2,1,0:T(8,128)}, f32[2]{0:T(128)}) custom-call(f32[8,64,128]{2,1,0:T(8,128)S(1)} %get-tuple-element.8.den, f32[3,8,64,128]{3,2,1,0:T(8,128)S(1)} %get-tuple-element.9.mom, f32[8,64,128]{2,1,0:T(8,128)S(1)} %get-tuple-element.10.en, ...), custom_call_target="tpu_custom_call" | custom-call | tf_op jit(solution)/shard_map/pallas_call | solution.py:535
